TPU v7x, 32 devices: a whole 2x2x4 slice. The times are simulated.
32 devices in a mesh: row: 8 (over y, x, core), col: 4 (over z).
Axes of the slice: x: 2, y: 2, z: 4, core: 2. Of those that a mesh axis runs over, the one named last changes fastest.
Arguments:
- sources: float32 [3, 1024, 4096], P(None, 'row', 'col'), may hold values from -32 to 32
- labels: int32 [1024, 4096], P('row', 'col'), may hold values from 0 to 2
Outputs:
- blended: float32 [1024, 4096], P('row', 'col')
- overview_fine: float32 [512, 2048], P('row', 'col')
- overview_mid: float32 [256, 1024], P(None, 'col')
- overview_coarse: float32 [128, 512], P(None, 'col')
All inputs are finite; a program needn't handle non-finite values.
Results may differ from a plain program's by a relative error of at most 0.0001.
Values sent between devices are 32-bit elements; how exact they have to be, the bound alone decides.
A program may use at most 64 MiB of HBM per device.

v0:
```python
import functools

import jax
import jax.numpy as jnp
from jax import lax
from jax.experimental import pallas as pl
from jax.experimental.pallas import tpu as pltpu
from jax.sharding import PartitionSpec as P

ITERS = 3
MESH = pl.DeviceIdType.MESH
HALO = 4
TOP = 16
SIDES = ((-1, 0), (1, 0), (0, -1), (0, 1), (-1, -1), (-1, 1), (1, -1), (1, 1))


def load_strip(ref, index, start, lanes):
    start = start if isinstance(start, int) else pl.multiple_of(start, 8)
    parts = [ref[index + (pl.ds(start, 8), pl.ds(first, size))] for first, size in lanes]
    return parts[0] if len(parts) == 1 else jnp.concatenate(parts, axis=1)


def neighbour_sum(ref, index, start, lanes, mid):
    width = mid.shape[1]
    above = load_strip(ref, index, start - 8, lanes)
    below = load_strip(ref, index, start + 8, lanes)
    sub = lax.broadcasted_iota(jnp.int32, mid.shape, 0)
    up = pltpu.roll(jnp.where(sub == 7, above, mid), 1, axis=0)
    down = pltpu.roll(jnp.where(sub == 0, below, mid), 7, axis=0)
    left = pltpu.roll(mid, 1, axis=1)
    right = pltpu.roll(mid, width - 1, axis=1)
    return (up + down) + (left + right)


def fold_lanes(strip, cols):
    total = strip[:, 0:128]
    for tile in range(1, cols // 128):
        total = total + strip[:, tile * 128:(tile + 1) * 128]
    return total


def quadratic(left, right, moments, shift):
    total = None
    for i, a in enumerate(left):
        for j, b in enumerate(right):
            term = a * b * moments[i + j + shift]
            total = term if total is None else total + term
    return total


def padded_sum(a, b):
    if len(a) < len(b):
        a, b = b, a
    return [x + b[i] if i < len(b) else x for i, x in enumerate(a)]


def coefficients(moments):
    residual = [jnp.ones_like(moments[0])]
    direction = residual
    solution_coords = [jnp.zeros_like(moments[0])]
    norm_now = moments[0]
    for iteration in range(ITERS):
        applied_dot = 4.0 * (
            quadratic(direction, direction, moments, 0)
            - quadratic(direction, direction, moments, 1)
        )
        step = norm_now / applied_dot
        solution_coords = padded_sum(solution_coords, [step * d for d in direction])
        if iteration + 1 < ITERS:
            moved = [-4.0 * step * d for d in direction]
            residual = padded_sum(residual, moved)
            residual = padded_sum(residual, [jnp.zeros_like(step)] + [-m for m in moved])
            norm_next = quadratic(residual, residual, moments, 0)
            ratio = norm_next / norm_now
            direction = padded_sum(residual, [ratio * d for d in direction])
            norm_now = norm_next
    return solution_coords


def pooled(values, half, slot, pool, stride):
    total = None
    for _ in range(3):
        piece = values.astype(jnp.bfloat16)
        values = values - piece.astype(jnp.float32)
        part = jnp.dot(piece, pool, preferred_element_type=jnp.float32)
        total = part if total is None else total + part
    lines = values.shape[0]
    half[slot, 0:lines, :] = total
    result = half[slot, pl.ds(0, lines // stride, stride=stride), :]
    for line in range(1, stride):
        result = result + half[slot, pl.ds(line, lines // stride, stride=stride), :]
    return result


def pool_matrix(stride):
    shape = (128 * stride, 128)
    source, target = (lax.broadcasted_iota(jnp.int32, shape, d) for d in range(2))
    return jnp.where(source // stride == target, 1.0 / (stride * stride), 0.0).astype(jnp.bfloat16)


def gather_kernel(
    n_row, n_col, rows, cols, kinds,
    src_hbm, lab_hbm, vec, mids, coord_ref,
    src, lab, mask, pack_r, pack_c, got_r, got_c, got_d, moment, half,
    load_sem, send_sem, recv_sem, mom_send, mom_recv, mid_send, mid_recv, fwd_send, fwd_recv,
):
    width = cols + 128
    n = n_row * n_col
    row, col = lax.axis_index("row"), lax.axis_index("col")
    me = row * n_col + col
    loads = [
        pltpu.make_async_copy(
            src_hbm.at[k], src.at[k, pl.ds(TOP, rows), pl.ds(0, cols)], load_sem.at[k]
        )
        for k in range(kinds)
    ]
    loads.append(
        pltpu.make_async_copy(lab_hbm, lab.at[pl.ds(TOP, rows), pl.ds(0, cols)], load_sem.at[kinds])
    )
    for load in loads:
        load.start()

    barrier = pltpu.get_barrier_semaphore()

    columns = [col]
    for _ in range(n_col - 1):
        columns.append(jnp.where(columns[-1] + 1 == n_col, 0, columns[-1] + 1))

    def for_all_others(act):
        for c in columns[1:]:
            act(row, c)

        def body(step, _):
            r = row + step
            r = jnp.where(r >= n_row, r - n_row, r)
            for c in columns:
                act(r, c)
            return 0

        lax.fori_loop(1, n_row, body, 0)

    for_all_others(lambda r, c: pl.semaphore_signal(
        barrier, inc=1, device_id=(r, c), device_id_type=MESH))

    first_row, last_row = row == 0, row == n_row - 1
    first_col, last_col = col == 0, col == n_col - 1
    quarter = jnp.full((8, width), 0.25, jnp.float32)
    lane = lax.broadcasted_iota(jnp.int32, (8, width), 1)
    off = ((lane >= cols) & (lane < cols + 64) & last_col) | ((lane >= cols + 64) & first_col)
    inside = jnp.where(off, 0.0, quarter)
    mask[0] = jnp.where(first_row, 0.0, inside)
    mask[1] = inside
    mask[2] = jnp.where(last_row, 0.0, inside)
    zero = jnp.zeros((8, width), jnp.float32)
    for which in range(3):
        vec[which, 0:8] = zero
        vec[which, rows + 24:rows + 32] = zero

    for load in loads:
        load.wait()

    for k in range(kinds + 1):
        def edge(rng, lanes):
            if k < kinds:
                return src[k, rng, lanes]
            return lab[rng, lanes].astype(jnp.float32)

        at = slice(HALO * k, HALO * (k + 1))
        pack_r[0, at, :] = edge(pl.ds(TOP, HALO), pl.ds(0, cols))
        pack_r[1, at, :] = edge(pl.ds(TOP + rows - HALO, HALO), pl.ds(0, cols))
    n_pack = HALO * (kinds + 1)
    tile_lane = lax.broadcasted_iota(jnp.int32, (rows, 128), 1)
    packed = jnp.zeros((rows, 128), jnp.float32)
    for k in range(kinds + 1):
        for side in range(2):
            lanes = pl.ds(0 if side == 0 else cols - 128, 128)
            if k < kinds:
                tile = src[k, pl.ds(TOP, rows), lanes]
            else:
                tile = lab[pl.ds(TOP, rows), lanes].astype(jnp.float32)
            target = side * n_pack + HALO * k
            origin = 0 if side == 0 else 128 - HALO
            if (target - origin) % 128:
                tile = pltpu.roll(tile, (target - origin) % 128, axis=1)
            packed = jnp.where((tile_lane >= target) & (tile_lane < target + HALO), tile, packed)
    turned = jnp.transpose(packed)
    pack_c[0] = turned[0:n_pack]
    pack_c[1] = turned[n_pack:2 * n_pack]

    groups = rows // 8 + 2
    whole = ((0, width),)
    around = ((cols - 128, 256), (0, 128))

    def right_side(start, lanes):
        here = load_strip(lab, (), start, lanes)
        total = jnp.zeros(here.shape, jnp.float32)
        for k in range(kinds):
            mid = load_strip(src, (k,), start, lanes)
            term = 4.0 * mid - neighbour_sum(src, (k,), start, lanes, mid)
            total = jnp.where(here == k, term, total)
        return total

    def stage(which, g, lanes, share):
        start = g * 8
        if which == 0:
            return right_side(start, lanes)
        mid = load_strip(vec, (which - 1,), start, lanes)
        return load_strip(mask, (share,), 0, lanes) * neighbour_sum(
            vec, (which - 1,), start, lanes, mid)

    def inner(which):
        def body(g, _):
            vec[which, pl.ds(pl.multiple_of(g * 8, 8), 8), :] = stage(which, g, whole, 1)
            return 0

        lax.fori_loop(2, groups, body, 0, unroll=2)

    edge_lane = lax.broadcasted_iota(jnp.int32, (8, 128), 1)

    def frame(which):
        for g, share in ((1, 0), (2, 1), (groups - 1, 1), (groups, 2)):
            vec[which, pl.ds(g * 8, 8), :] = stage(which, g, whole, share)

        def body(g, _):
            lines = pl.ds(pl.multiple_of(g * 8, 8), 8)
            new = stage(which, g, around, 1)
            last = vec[which, lines, pl.ds(cols - 128, 128)]
            first = vec[which, lines, pl.ds(0, 128)]
            vec[which, lines, pl.ds(cols - 128, 128)] = jnp.where(
                edge_lane >= 64, new[:, 0:128], last)
            vec[which, lines, pl.ds(cols, 128)] = new[:, 128:256]
            vec[which, lines, pl.ds(0, 128)] = jnp.where(edge_lane < 64, new[:, 256:384], first)
            return 0

        lax.fori_loop(3, groups - 1, body, 0, unroll=2)

    inner(0)
    pl.semaphore_wait(barrier, n - 1)

    sends = []
    for i, (dr, dc) in enumerate(SIDES):
        if dc == 0:
            source = pack_r.at[0 if dr < 0 else 1]
            target = got_r.at[1 if dr < 0 else 0]
        elif dr == 0:
            source = pack_c.at[0 if dc < 0 else 1]
            target = got_c.at[1 if dc < 0 else 0]
        else:
            lanes = pl.ds(0 if dc < 0 else cols - 128, 128)
            source = pack_r.at[0 if dr < 0 else 1, :, lanes]
            target = got_d.at[1 if dr < 0 else 0, 1 if dc < 0 else 0]
        there = jnp.logical_and(
            jnp.logical_and(row + dr >= 0, row + dr < n_row),
            jnp.logical_and(col + dc >= 0, col + dc < n_col),
        )
        opposite = SIDES.index((-dr, -dc))
        device = (
            jnp.clip(row + dr, 0, n_row - 1),
            jnp.clip(col + dc, 0, n_col - 1),
        )
        copy = pltpu.make_async_remote_copy(
            src_ref=source, dst_ref=target, send_sem=send_sem.at[i],
            recv_sem=recv_sem.at[opposite], device_id=device, device_id_type=MESH,
        )
        back = pltpu.make_async_remote_copy(
            src_ref=source, dst_ref=got_r.at[0 if dr < 0 else 1] if dc == 0 else (
                got_c.at[0 if dc < 0 else 1] if dr == 0
                else got_d.at[0 if dr < 0 else 1, 0 if dc < 0 else 1]),
            send_sem=send_sem.at[i], recv_sem=recv_sem.at[i],
            device_id=device, device_id_type=MESH,
        )
        sends.append((there, copy, back))
        pl.when(there)(copy.start)
    for which in range(1, ITERS):
        inner(which)

    for there, copy, back in sends:
        pl.when(there)(back.wait_recv)

    halo_lane = lax.broadcasted_iota(jnp.int32, (HALO, 128), 1)
    for side in range(2):
        missing_row = first_row if side == 0 else last_row
        base = TOP - HALO if side == 0 else TOP + rows
        other = TOP - 8 if side == 0 else TOP + rows + HALO
        for k in range(kinds + 1):
            fill = jnp.float32(0.0 if k < kinds else -1.0)
            at = slice(HALO * k, HALO * (k + 1))
            wide = jnp.where(missing_row, fill, got_r[side, at, :])
            right = jnp.where(
                (halo_lane < HALO) & jnp.logical_not(missing_row | last_col),
                got_d[side, 1, at, :], fill)
            corner = jnp.where(
                (halo_lane >= 128 - HALO) & jnp.logical_not(missing_row | first_col),
                got_d[side, 0, at, :], right)
            empty = jnp.full((HALO, width), fill)
            if k < kinds:
                src[k, pl.ds(base, HALO), pl.ds(0, cols)] = wide
                src[k, pl.ds(base, HALO), pl.ds(cols, 128)] = corner
                src[k, pl.ds(other, HALO), :] = empty
            else:
                lab[pl.ds(base, HALO), pl.ds(0, cols)] = wide.astype(jnp.int32)
                lab[pl.ds(base, HALO), pl.ds(cols, 128)] = corner.astype(jnp.int32)
                lab[pl.ds(other, HALO), :] = empty.astype(jnp.int32)
    both = jnp.concatenate(
        [
            got_c[1],
            got_c[0],
            jnp.zeros((128 - 2 * n_pack, rows), jnp.float32),
        ],
        axis=0,
    )
    unturned = jnp.transpose(both)
    for k in range(kinds + 1):
        fill = jnp.float32(0.0 if k < kinds else -1.0)
        right = pltpu.roll(unturned, (-HALO * k) % 128, axis=1)
        left = pltpu.roll(unturned, (128 - HALO - n_pack - HALO * k) % 128, axis=1)
        tile = jnp.where((tile_lane < HALO) & jnp.logical_not(last_col), right, fill)
        tile = jnp.where((tile_lane >= 128 - HALO) & jnp.logical_not(first_col), left, tile)
        if k < kinds:
            src[k, pl.ds(TOP, rows), pl.ds(cols, 128)] = tile
        else:
            lab[pl.ds(TOP, rows), pl.ds(cols, 128)] = tile.astype(jnp.int32)

    chips = n_row // 2
    partner = row + 1 - 2 * lax.rem(row, 2)
    quad = rows // 4
    pool = pool_matrix(4)

    def block(w, owner):
        return mids.at[w, pl.ds(pl.multiple_of(owner * quad, 8), quad)]

    def peer(step):
        other = row + 2 * step
        return jnp.where(other >= n_row, other - n_row, other)

    def hand(w, owner, target, send, recv):
        return pltpu.make_async_remote_copy(
            src_ref=block(w, owner), dst_ref=block(w, owner), send_sem=send, recv_sem=recv,
            device_id=(target, col), device_id_type=MESH)

    def gather(w):
        for tile in range(cols // 512):
            mids[w, pl.ds(pl.multiple_of(row * quad, 8), quad), pl.ds(tile * 128, 128)] = pooled(
                vec[w, pl.ds(TOP, rows), pl.ds(tile * 512, 512)], half,
                w * (cols // 512) + tile, pool, 4)
        hops = [
            hand(w, row, peer(step), mid_send.at[w, step], mid_recv.at[w, step])
            for step in range(1, chips)
        ]
        hops.append(hand(w, row, partner, mid_send.at[w, 0], mid_recv.at[w, 0]))
        for hop in hops:
            hop.start()
        return hops

    hops = []
    frame(0)
    for which in range(ITERS - 1):
        hops += gather(which)
        frame(which + 1)

    def products(g, sums):
        start = pl.multiple_of(g * 8, 8)
        powers = [vec[w, pl.ds(start, 8), :] for w in range(ITERS)]
        powers.append(0.25 * neighbour_sum(vec, (ITERS - 1,), start, whole, powers[-1]))
        return tuple(
            s + fold_lanes(powers[i // 2] * powers[(i + 1) // 2], cols)
            for i, s in enumerate(sums)
        )

    sums = lax.fori_loop(
        2, groups, products, tuple(jnp.zeros((8, 128), jnp.float32) for _ in range(2 * ITERS)), unroll=2)
    lane1 = lax.broadcasted_iota(jnp.int32, (1, 128), 1)
    mine = jnp.zeros((1, 128), jnp.float32)
    for i, s in enumerate(sums):
        mine = jnp.where(lane1 == i, jnp.sum(s, keepdims=True), mine)
    moment[me] = mine

    for_all_others(lambda r, c: pltpu.make_async_remote_copy(
        src_ref=moment.at[me], dst_ref=moment.at[me], send_sem=mom_send, recv_sem=mom_recv,
        device_id=(r, c), device_id_type=MESH).start())
    hops += gather(ITERS - 1)
    everyone = moment.at[pl.ds(0, n - 1)]
    pltpu.make_async_copy(everyone, everyone, mom_recv).wait()
    total = jnp.sum(moment[...], axis=0)
    moments = [
        jnp.sum(jnp.where(lane1 == i, total, 0.0), axis=1, keepdims=True) for i in range(2 * ITERS)
    ]
    for w, c in enumerate(coefficients(moments)):
        coord_ref[w] = jnp.broadcast_to(c, (8, 128))

    def source_of(step):
        other = row - 2 * step
        return jnp.where(other < 0, other + n_row, other)

    def other_core(owner):
        return owner + 1 - 2 * lax.rem(owner, 2)

    forwards = []
    for w in range(ITERS):
        for step in range(1, chips):
            owner = source_of(step)
            hand(w, owner, partner, mid_send.at[w, step], mid_recv.at[w, step]).wait_recv()
            forward = hand(w, owner, partner, fwd_send.at[w, step], fwd_recv.at[w, step])
            forward.start()
            forwards.append(forward)
    for w in range(ITERS):
        hand(w, partner, partner, mid_send.at[w, 0], mid_recv.at[w, 0]).wait_recv()
        for step in range(1, chips):
            hand(w, other_core(source_of(step)), partner,
                 fwd_send.at[w, step], fwd_recv.at[w, step]).wait_recv()
    for hop in hops:
        hop.wait_send()
    for forward in forwards:
        forward.wait_send()
    for there, copy, back in sends:
        pl.when(there)(copy.wait_send)
    pltpu.make_async_copy(everyone, everyone, mom_send).wait()


def finish_kernel(
    rows, cols, vec, mids, coord_ref, blend_out, fine_out, mid_out, coarse_out,
    blend, fine, mid, coarse, half, out_sem,
):
    pool = pool_matrix(2)

    def leave(slot, source, target):
        copy = pltpu.make_async_copy(source, target, out_sem.at[slot])
        copy.start()
        return copy

    def combine(source, target, lines, lanes, first):
        coords = [jnp.concatenate([coord_ref[w]] * (lanes // 128), axis=1) for w in range(ITERS)]

        def body(g, _):
            start = pl.multiple_of(g * 8, 8)
            strip = None
            for w in range(ITERS):
                term = coords[w] * source[w, pl.ds(start + first, 8), pl.ds(0, lanes)]
                strip = term if strip is None else strip + term
            target[pl.ds(start, 8), :] = strip
            return 0

        lax.fori_loop(0, lines // 8, body, 0, unroll=4)

    combine(vec, blend, rows, cols, TOP)
    copies = [leave(0, blend, blend_out)]
    tall, wide = mid.shape
    combine(mids, mid, tall, wide, 0)
    copies.append(leave(1, mid, mid_out))
    for tile in range(cols // 256):
        fine[:, tile * 128:(tile + 1) * 128] = pooled(
            blend[:, tile * 256:(tile + 1) * 256], half, tile, pool, 2)
    copies.append(leave(2, fine, fine_out))
    for tile in range(wide // 256):
        coarse[:, tile * 128:(tile + 1) * 128] = pooled(
            mid[:, tile * 256:(tile + 1) * 256], half, cols // 256 + tile, pool, 2)
    copies.append(leave(3, coarse, coarse_out))
    for copy in copies:
        copy.wait()


def per_device(n_row, n_col, sources, labels):
    kinds, rows, cols = sources.shape
    n = n_row * n_col
    tall, width = rows + 32, cols + 128
    n_pack = HALO * (kinds + 1)
    f32 = jnp.float32
    vmem = pl.BlockSpec(memory_space=pltpu.VMEM)
    hbm = pl.BlockSpec(memory_space=pltpu.HBM)
    mid_shape = (n_row * rows // 4, cols // 4)
    coarse_shape = (n_row * rows // 8, cols // 8)
    chips = n_row // 2
    dma = pltpu.SemaphoreType.DMA
    vec, mids, coords = pl.pallas_call(
        functools.partial(gather_kernel, n_row, n_col, rows, cols, kinds),
        out_shape=(
            jax.ShapeDtypeStruct((ITERS, tall, width), f32),
            jax.ShapeDtypeStruct((ITERS,) + mid_shape, f32),
            jax.ShapeDtypeStruct((ITERS, 8, 128), f32),
        ),
        in_specs=[hbm] * 2,
        out_specs=(vmem,) * 3,
        scratch_shapes=[
            pltpu.VMEM((kinds, tall, width), f32),
            pltpu.VMEM((tall, width), jnp.int32),
            pltpu.VMEM((3, 8, width), f32),
            pltpu.VMEM((2, n_pack, cols), f32),
            pltpu.VMEM((2, n_pack, rows), f32),
            pltpu.VMEM((2, n_pack, cols), f32),
            pltpu.VMEM((2, n_pack, rows), f32),
            pltpu.VMEM((2, 2, n_pack, 128), f32),
            pltpu.VMEM((n, 1, 128), f32),
            pltpu.VMEM((ITERS * (cols // 512), rows, 128), f32),
            dma((kinds + 1,)),
            dma((8,)),
            dma((8,)),
            dma,
            dma,
            dma((ITERS, chips)),
            dma((ITERS, chips)),
            dma((ITERS, chips)),
            dma((ITERS, chips)),
        ],
        compiler_params=pltpu.CompilerParams(
            collective_id=0, has_side_effects=True, vmem_limit_bytes=20 * 2**20),
    )(
        pltpu.with_memory_space_constraint(sources, pltpu.HBM),
        pltpu.with_memory_space_constraint(labels, pltpu.HBM),
    )
    return pl.pallas_call(
        functools.partial(finish_kernel, rows, cols),
        out_shape=(
            jax.ShapeDtypeStruct((rows, cols), f32),
            jax.ShapeDtypeStruct((rows // 2, cols // 2), f32),
            jax.ShapeDtypeStruct(mid_shape, f32),
            jax.ShapeDtypeStruct(coarse_shape, f32),
        ),
        in_specs=[vmem] * 3,
        out_specs=(hbm,) * 4,
        scratch_shapes=[
            pltpu.VMEM((rows, cols), f32),
            pltpu.VMEM((rows // 2, cols // 2), f32),
            pltpu.VMEM(mid_shape, f32),
            pltpu.VMEM(coarse_shape, f32),
            pltpu.VMEM((cols // 256 + cols // 1024, max(rows, mid_shape[0]), 128), f32),
            dma((4,)),
        ],
        compiler_params=pltpu.CompilerParams(vmem_limit_bytes=20 * 2**20),
    )(vec, mids, coords)


def solution(mesh):
    sizes = dict(mesh.shape)
    return jax.shard_map(
        functools.partial(per_device, sizes["row"], sizes["col"]),
        mesh=mesh,
        in_specs=(P(None, "row", "col"), P("row", "col")),
        out_specs=(P("row", "col"), P("row", "col"), P(None, "col"), P(None, "col")),
        check_vma=False,
    )
```

profile of v0, /device:TPU:0, one launch (start us, length us, event | category | flops | bytes accessed | tf_op | source)
XLA Modules:
  0.0 24.8 jit_solution(12651590104172584685)
XLA Ops:
  0.6 22.7 %shard_map.57 = (f32[3,160,1152]{2,1,0:T(8,128)S(1)}, f32[3,256,256]{2,1,0:T(8,128)S(1)}, f32[3,8,128]{2,1,0:T(8,128)S(1)}) custom-call(f32[3,128,1024]{2,1,0:T(8,128)} %src_hbm.1, s32[128,1024]{1,0:T(8,128)} %lab_hbm.1), custom_call_target="tpu_custom_call" | custom-call | tf_op jit(solution)/shard_map/pallas_call | solution.py:474
  23.4 1.4 %shard_map.58 = (f32[128,1024]{1,0:T(8,128)}, f32[64,512]{1,0:T(8,128)}, f32[256,256]{1,0:T(8,128)}, f32[128,128]{1,0:T(8,128)}) custom-call(f32[3,160,1152]{2,1,0:T(8,128)S(1)} %get-tuple-element.7.vec, f32[3,256,256]{2,1,0:T(8,128)S(1)} %get-tuple-element.8.mids, f32[3,8,128]{2,1,0:T(8,128)S(1)} %get-tuple-element.9.coord_ref), custom_call_target="tpu_custom_call" | custom-call | tf_op jit(solution)/shard_map/pallas_call | solution.py:510
where the time goes:
time: 25 us; the launch traced here: 24.8 us
  Pallas kernels  24.2 us (97%)
  between operations  0.64 us (3%)
    pallas_call x1, Pallas kernels, per_device(): pl.pallas_call(functools.partial(gather_kernel, n_row, n_col, rows, cols,...  22.7 us
    pallas_call x1, Pallas kernels, per_device(): pl.pallas_call(functools.partial(finish_kernel, rows, cols), out_shape=(j...  1.44 us

commit v1 on v0

v1 whole, which is shorter than its diff:
```python
import functools

import jax
import jax.numpy as jnp
from jax import lax
from jax.experimental import pallas as pl
from jax.experimental.pallas import tpu as pltpu
from jax.sharding import PartitionSpec as P

ITERS = 3
MESH = pl.DeviceIdType.MESH
HALO = 4
TOP = 8
LANES = 128
SIDES = ((-1, -1), (-1, 1), (1, -1), (1, 1), (-1, 0), (1, 0), (0, -1), (0, 1))


def lane_of(shape):
    return lax.broadcasted_iota(jnp.int32, shape, len(shape) - 1)


def line_of(shape):
    return lax.broadcasted_iota(jnp.int32, shape, len(shape) - 2)


def lines(ref, index, start):
    return ref[index + (pl.ds(start, 8), slice(None))]


def beside_ring(mid):
    tiles = mid.shape[0]
    lane = lane_of(mid.shape)
    left = pltpu.roll(mid, 1, axis=2)
    right = pltpu.roll(mid, LANES - 1, axis=2)
    from_left = jnp.concatenate([left[tiles - 1:], left[:tiles - 1]], axis=0)
    from_right = jnp.concatenate([right[1:], right[:1]], axis=0)
    return jnp.where(lane == 0, from_left, left) + jnp.where(lane == LANES - 1, from_right, right)


def beside_tile(mid):
    return pltpu.roll(mid, 1, axis=1) + pltpu.roll(mid, LANES - 1, axis=1)


def neighbour_sum(ref, index, start, mid, beside):
    return (lines(ref, index, start - 1) + lines(ref, index, start + 1)) + beside(mid)


def right_side(src, lab, tile, start, beside):
    here = lines(lab, (tile,), start)
    total = None
    for k in reversed(range(src.shape[0])):
        mid = lines(src, (k, tile), start)
        term = 4.0 * mid - neighbour_sum(src, (k, tile), start, mid, beside)
        total = term if total is None else jnp.where(here == k, term, total)
    return total


def quadratic(left, right, moments, shift):
    total = None
    for i, a in enumerate(left):
        for j, b in enumerate(right):
            term = a * b * moments[i + j + shift]
            total = term if total is None else total + term
    return total


def padded_sum(a, b):
    if len(a) < len(b):
        a, b = b, a
    return [x + b[i] if i < len(b) else x for i, x in enumerate(a)]


def coefficients(moments):
    residual = [jnp.ones_like(moments[0])]
    direction = residual
    solution_coords = [jnp.zeros_like(moments[0])]
    norm_now = moments[0]
    for iteration in range(ITERS):
        applied_dot = 4.0 * (
            quadratic(direction, direction, moments, 0)
            - quadratic(direction, direction, moments, 1)
        )
        step = norm_now / applied_dot
        solution_coords = padded_sum(solution_coords, [step * d for d in direction])
        if iteration + 1 < ITERS:
            moved = [-4.0 * step * d for d in direction]
            residual = padded_sum(residual, moved)
            residual = padded_sum(residual, [jnp.zeros_like(step)] + [-m for m in moved])
            norm_next = quadratic(residual, residual, moments, 0)
            ratio = norm_next / norm_now
            direction = padded_sum(residual, [ratio * d for d in direction])
            norm_now = norm_next
    return solution_coords


def split_dot(values, pool):
    total = None
    for _ in range(3):
        piece = values.astype(jnp.bfloat16)
        values = values - piece.astype(jnp.float32)
        part = jnp.dot(piece, pool, preferred_element_type=jnp.float32)
        total = part if total is None else total + part
    return total


def pooled(load, stride, pool):
    parts = []
    for tile in range(stride):
        part = load(tile, 0)
        for line in range(1, stride):
            part = part + load(tile, line)
        parts.append(part)
    return split_dot(jnp.concatenate(parts, axis=1), pool)


def pool_matrix(stride):
    shape = (LANES * stride, LANES)
    source, target = (lax.broadcasted_iota(jnp.int32, shape, d) for d in range(2))
    return jnp.where(source // stride == target, 1.0 / (stride * stride), 0.0).astype(jnp.bfloat16)


def gather_kernel(
    n_row, n_col, rows, cols, kinds,
    src_hbm, lab_hbm, vec, fines, mids, coord_ref,
    src, lab, edge, edge_lab, pack_r, pack_c, got_r, got_c, got_d, part, moment,
    load_sem, send_sem, recv_sem, mom_send, mom_recv, mid_send, mid_recv, fwd_send, fwd_recv,
):
    tiles = cols // LANES
    side_tile = tiles
    main = slice(0, tiles)
    body_rows = pl.ds(TOP, rows)
    n = n_row * n_col
    row, col = lax.axis_index("row"), lax.axis_index("col")
    me = row * n_col + col
    f32 = jnp.float32

    def plane_load(k, t):
        lanes = pl.ds(t * LANES, LANES)
        if k < kinds:
            return pltpu.make_async_copy(
                src_hbm.at[k, :, lanes], src.at[k, t, body_rows], load_sem.at[k, t])
        return pltpu.make_async_copy(lab_hbm.at[:, lanes], lab.at[t, body_rows], load_sem.at[k, t])

    def edge_load(k, side):
        here = pl.ds(0 if side == 0 else rows - 8, 8)
        if k < kinds:
            return pltpu.make_async_copy(
                src_hbm.at[k, here], edge.at[k, side], load_sem.at[k, tiles + side])
        return pltpu.make_async_copy(lab_hbm.at[here], edge_lab.at[side], load_sem.at[k, tiles + side])

    first_loads = [plane_load(k, t) for k in range(kinds + 1) for t in (0, tiles - 1)]
    first_loads += [edge_load(k, side) for k in range(kinds + 1) for side in range(2)]
    later_loads = [plane_load(k, t) for t in range(1, tiles - 1) for k in range(kinds + 1)]
    for load in first_loads:
        load.start()

    barrier = pltpu.get_barrier_semaphore()

    columns = [col]
    for _ in range(n_col - 1):
        columns.append(jnp.where(columns[-1] + 1 == n_col, 0, columns[-1] + 1))

    def for_all_others(act):
        for c in columns[1:]:
            act(row, c)

        def body(step, _):
            r = row + step
            r = jnp.where(r >= n_row, r - n_row, r)
            for c in columns:
                act(r, c)
            return 0

        lax.fori_loop(1, n_row, body, 0)

    for_all_others(lambda r, c: pl.semaphore_signal(
        barrier, inc=1, device_id=(r, c), device_id_type=MESH))
    for load in later_loads:
        load.start()

    first_row, last_row = row == 0, row == n_row - 1
    first_col, last_col = col == 0, col == n_col - 1
    pad = jnp.zeros((tiles + 1, 8, LANES), f32)
    for start in (0, TOP + rows):
        for k in range(kinds):
            src[k, :, pl.ds(start, 8), :] = pad
        lab[:, pl.ds(start, 8), :] = pad.astype(jnp.int32)
        for w in range(ITERS):
            vec[w, :, pl.ds(start, 8), :] = pad

    n_pack = HALO * (kinds + 1)
    with jax.named_scope("wait_first"):
        for load in first_loads:
            load.wait()
    with jax.named_scope("pack"):
        for k in range(kinds + 1):
            at = pl.ds(HALO * k, HALO)
            for side in range(2):
                lines_here = pl.ds(0 if side == 0 else 8 - HALO, HALO)
                for t in range(tiles):
                    lanes = pl.ds(t * LANES, LANES)
                    if k < kinds:
                        value = edge[k, side, lines_here, lanes]
                    else:
                        value = edge_lab[side, lines_here, lanes].astype(f32)
                    pack_r[side, t, at, :] = value
        wide_lane = lane_of((rows, LANES))
        for k in range(kinds + 1):
            if k < kinds:
                first, last = src[k, 0, body_rows], src[k, tiles - 1, body_rows]
            else:
                first, last = lab[0, body_rows].astype(f32), lab[tiles - 1, body_rows].astype(f32)
            both = jnp.where(wide_lane < LANES // 2, first, last)
            turned = jnp.transpose(both)
            at = pl.ds(HALO * k, HALO)
            pack_c[0, at, :] = turned[0:HALO]
            pack_c[1, at, :] = turned[LANES - HALO:LANES]

    with jax.named_scope("barrier"):
        pl.semaphore_wait(barrier, n - 1)

    sends = []
    for i, (dr, dc) in enumerate(SIDES):
        mine_r, mine_c = (0 if dr < 0 else 1), (0 if dc < 0 else 1)
        if dc == 0:
            source, target, here = pack_r.at[mine_r], got_r.at[1 - mine_r], got_r.at[mine_r]
        elif dr == 0:
            source, target, here = pack_c.at[mine_c], got_c.at[1 - mine_c], got_c.at[mine_c]
        else:
            source = pack_r.at[mine_r, 0 if dc < 0 else tiles - 1]
            target, here = got_d.at[1 - mine_r, 1 - mine_c], got_d.at[mine_r, mine_c]
        there = jnp.logical_and(
            jnp.logical_and(row + dr >= 0, row + dr < n_row),
            jnp.logical_and(col + dc >= 0, col + dc < n_col),
        )
        opposite = SIDES.index((-dr, -dc))
        device = (
            jnp.clip(row + dr, 0, n_row - 1),
            jnp.clip(col + dc, 0, n_col - 1),
        )
        copy = pltpu.make_async_remote_copy(
            src_ref=source, dst_ref=target, send_sem=send_sem.at[i],
            recv_sem=recv_sem.at[opposite], device_id=device, device_id_type=MESH,
        )
        back = pltpu.make_async_remote_copy(
            src_ref=source, dst_ref=here, send_sem=send_sem.at[i],
            recv_sem=recv_sem.at[i], device_id=device, device_id_type=MESH,
        )
        sends.append((there, copy, back))
        pl.when(there)(copy.start)

    with jax.named_scope("wait_later"):
        for load in later_loads:
            load.wait()
    groups = rows // 8
    lane_r = lane_of((tiles, 8, LANES))
    lane_t = lane_of((8, LANES))
    line_t = line_of((8, LANES))

    def whole_loop(count, act):
        def body(i, _):
            act(i)
            return 0

        lax.fori_loop(0, count, body, 0, unroll=count)

    def save(which, tile, start, value):
        vec[which, tile, pl.ds(start, 8), :] = value

    def applied(which, tile, start, beside):
        mid = lines(vec, (which, tile), start)
        return neighbour_sum(vec, (which, tile), start, mid, beside)

    with jax.named_scope("main_b"):
        whole_loop(groups, lambda i: save(
            0, main, TOP + 8 * i, right_side(src, lab, main, TOP + 8 * i, beside_ring)))
    with jax.named_scope("main_v"):
        for which in range(1, ITERS):
            whole_loop(groups, lambda i: save(
                which, main, TOP + 8 * i, applied(which - 1, main, TOP + 8 * i, beside_ring)))

    def products(tile, start, beside, keep):
        powers = [lines(vec, (w, tile), start) for w in range(ITERS)]
        powers.append(neighbour_sum(vec, (ITERS - 1, tile), start, powers[-1], beside))
        kept = [keep(p) for p in powers[:ITERS]]
        return [kept[i // 2] * powers[(i + 1) // 2] for i in range(2 * ITERS)]

    def keep_main(p):
        edge_lane = lane_of((1, 8, LANES))
        return jnp.concatenate([
            jnp.where(edge_lane < HALO, 0.0, p[0:1]), p[1:tiles - 1],
            jnp.where(edge_lane >= LANES - HALO, 0.0, p[tiles - 1:]),
        ], axis=0)

    def fold(value):
        if len(value.shape) == 2:
            return value
        total = value[0]
        for t in range(1, value.shape[0]):
            total = total + value[t]
        return total

    with jax.named_scope("main_m"):
        def main_body(i, sums):
            new = products(main, TOP + HALO + 8 * i, beside_ring, keep_main)
            return tuple(s + fold(p) for s, p in zip(sums, new))

        zero8 = jnp.zeros((8, LANES), f32)
        sums = lax.fori_loop(
            0, groups - 1, main_body, tuple(zero8 for _ in range(2 * ITERS)), unroll=groups - 1)
        for i, s in enumerate(sums):
            part[i] = s
    with jax.named_scope("side_fill"):
        for k in range(kinds + 1):
            if k < kinds:
                first, last = src[k, 0, body_rows], src[k, tiles - 1, body_rows]
                src[k, side_tile, body_rows, :] = jnp.where(
                    wide_lane < LANES // 2, pltpu.roll(first, 2 * HALO, axis=1), last)
            else:
                first, last = lab[0, body_rows], lab[tiles - 1, body_rows]
                lab[side_tile, body_rows, :] = jnp.where(
                    wide_lane < LANES // 2, pltpu.roll(first, 2 * HALO, axis=1), last)

    with jax.named_scope("wait_halo"):
        for there, copy, back in sends:
            pl.when(there)(back.wait_recv)

    with jax.named_scope("unpack"):
        for k in range(kinds + 1):
            at = pl.ds(HALO * k, HALO)
            right = jnp.where(last_col, 0.0, got_c[1, at, :])
            left = jnp.where(first_col, 0.0, got_c[0, at, :])
            turned = jnp.transpose(jnp.concatenate([right, left], axis=0))
            if k < kinds:
                src[k, side_tile, body_rows, 0:2 * HALO] = turned
            else:
                lab[side_tile, body_rows, 0:2 * HALO] = turned.astype(jnp.int32)
        corner_lane = lane_of((HALO, LANES))
        for side in range(2):
            missing = first_row if side == 0 else last_row
            base = TOP - HALO if side == 0 else TOP + rows
            for k in range(kinds + 1):
                at = pl.ds(HALO * k, HALO)
                wide = [jnp.where(missing, 0.0, got_r[side, t, at, :]) for t in range(tiles)]
                right = jnp.where(missing | last_col, 0.0, got_d[side, 1, at, :])
                left = jnp.where(missing | first_col, 0.0, got_d[side, 0, at, :])
                moved = pltpu.roll(
                    jnp.where(corner_lane >= LANES - HALO, left, wide[0]), 2 * HALO, axis=1)
                own = jnp.where(corner_lane < LANES // 2, moved, wide[-1])
                wide.append(jnp.where(corner_lane < HALO, right, own))
                for t, value in enumerate(wide):
                    if k < kinds:
                        src[k, t, pl.ds(base, HALO), :] = value
                    else:
                        lab[t, pl.ds(base, HALO), :] = value.astype(jnp.int32)

    off_lane = ((lane_t < HALO) & last_col) | ((lane_t >= HALO) & (lane_t < 2 * HALO) & first_col)
    off_top = (line_t < HALO) & first_row
    off_bottom = (line_t >= HALO) & last_row
    ends = ((TOP - HALO, off_top), (TOP + rows - HALO, off_bottom))

    def frame(which):
        def value(tile, start, beside):
            if which == 0:
                return right_side(src, lab, tile, start, beside)
            return applied(which - 1, tile, start, beside)

        def side_group(start, off):
            save(which, side_tile, start, jnp.where(off, 0.0, value(side_tile, start, beside_tile)))

        side_group(ends[0][0], off_top | off_lane)
        whole_loop(groups - 1, lambda i: side_group(TOP + HALO + 8 * i, off_lane))
        side_group(ends[1][0], off_bottom | off_lane)
        for start, off in ends:
            save(which, main, start, jnp.where(off[None], 0.0, value(main, start, beside_ring)))

    with jax.named_scope("frames"):
        for which in range(ITERS):
            frame(which)

    with jax.named_scope("moments"):
        sums = [part[i] for i in range(2 * ITERS)]
        on_side = ((lane_t >= 2 * HALO) & (lane_t < 3 * HALO)) | (lane_t >= LANES - HALO)

        def side_body(i, sums):
            new = products(
                side_tile, TOP + 8 * i, beside_tile, lambda p: jnp.where(on_side, p, 0.0))
            return tuple(s + p for s, p in zip(sums, new))

        sums = lax.fori_loop(0, groups, side_body, tuple(sums), unroll=groups)
        for (start, _), on in zip(ends, (line_t >= HALO, line_t < HALO)):
            new = products(main, start, beside_ring, lambda p: jnp.where(on[None], keep_main(p), 0.0))
            sums = [s + fold(p) for s, p in zip(sums, new)]
        lane1 = lane_of((1, LANES))
        mine = jnp.zeros((1, LANES), f32)
        for i, s in enumerate(sums):
            mine = jnp.where(lane1 == i, jnp.sum(s, keepdims=True), mine)
        moment[me] = mine

    with jax.named_scope("send_moments"):
        for_all_others(lambda r, c: pltpu.make_async_remote_copy(
            src_ref=moment.at[me], dst_ref=moment.at[me], send_sem=mom_send, recv_sem=mom_recv,
            device_id=(r, c), device_id_type=MESH).start())

    chips = n_row // 2
    partner = row + 1 - 2 * lax.rem(row, 2)
    quad = rows // 4
    pool4, pool2 = pool_matrix(4), pool_matrix(2)

    def block(w, owner):
        return mids.at[w, :, pl.ds(pl.multiple_of(owner * quad, 8), quad)]

    def peer(step):
        other = row + 2 * step
        return jnp.where(other >= n_row, other - n_row, other)

    def hand(w, owner, target, send, recv):
        return pltpu.make_async_remote_copy(
            src_ref=block(w, owner), dst_ref=block(w, owner), send_sem=send, recv_sem=recv,
            device_id=(target, col), device_id_type=MESH)

    hops = []
    with jax.named_scope("mids"):
        for w in range(ITERS):
            side = vec[w, side_tile, body_rows]
            vec[w, 0, body_rows, :] = jnp.where(
                wide_lane < HALO, pltpu.roll(side, LANES - 2 * HALO, axis=1), vec[w, 0, body_rows])
            vec[w, tiles - 1, body_rows, :] = jnp.where(
                wide_lane >= LANES - HALO, side, vec[w, tiles - 1, body_rows])
            for q in range(tiles // 4):
                mids[w, q, pl.ds(pl.multiple_of(row * quad, 8), quad), :] = pooled(
                    lambda tile, line: vec[w, 4 * q + tile, pl.ds(TOP + line, quad, stride=4), :],
                    4, pool4)
            here = [
                hand(w, row, peer(step), mid_send.at[w, step], mid_recv.at[w, step])
                for step in range(1, chips)
            ]
            here.append(hand(w, row, partner, mid_send.at[w, 0], mid_recv.at[w, 0]))
            for hop in here:
                hop.start()
            hops += here
    with jax.named_scope("fines"):
        for w in range(ITERS):
            for q in range(tiles // 2):
                fines[w, q] = pooled(
                    lambda tile, line: vec[
                        w, 2 * q + tile, pl.ds(TOP + line, rows // 2, stride=2), :],
                    2, pool2)

    with jax.named_scope("wait_moments"):
        everyone = moment.at[pl.ds(0, n - 1)]
        pltpu.make_async_copy(everyone, everyone, mom_recv).wait()
    with jax.named_scope("coefs"):
        total = jnp.sum(moment[...], axis=0)
        moments = [
            0.25 ** i * jnp.sum(jnp.where(lane1 == i, total, 0.0), axis=1, keepdims=True)
            for i in range(2 * ITERS)
        ]
        for w, c in enumerate(coefficients(moments)):
            coord_ref[w] = jnp.broadcast_to(0.25 ** w * c, (8, LANES))

    def source_of(step):
        other = row - 2 * step
        return jnp.where(other < 0, other + n_row, other)

    def other_core(owner):
        return owner + 1 - 2 * lax.rem(owner, 2)

    with jax.named_scope("forwards"):
        forwards = []
        for w in range(ITERS):
            for step in range(1, chips):
                owner = source_of(step)
                hand(w, owner, partner, mid_send.at[w, step], mid_recv.at[w, step]).wait_recv()
                forward = hand(w, owner, partner, fwd_send.at[w, step], fwd_recv.at[w, step])
                forward.start()
                forwards.append(forward)
    with jax.named_scope("wait_forwards"):
        for w in range(ITERS):
            hand(w, partner, partner, mid_send.at[w, 0], mid_recv.at[w, 0]).wait_recv()
            for step in range(1, chips):
                hand(w, other_core(source_of(step)), partner,
                     fwd_send.at[w, step], fwd_recv.at[w, step]).wait_recv()
    with jax.named_scope("wait_sends"):
        for hop in hops:
            hop.wait_send()
        for forward in forwards:
            forward.wait_send()
        for there, copy, back in sends:
            pl.when(there)(copy.wait_send)
        pltpu.make_async_copy(everyone, everyone, mom_send).wait()


def finish_kernel(
    rows, cols, vec, fines, mids, coord_ref, blend_out, fine_out, mid_out, coarse_out,
    blend, fine, mid, coarse, out_sem,
):
    tiles = cols // LANES
    started = []

    def leave(source, target):
        copy = pltpu.make_async_copy(source, target, out_sem.at[len(started)])
        copy.start()
        started.append(copy)

    def combine(load, target, height):
        coords = [coord_ref[w] for w in range(ITERS)]

        def body(g, _):
            start = pl.multiple_of(g * 8, 8)
            strip = None
            for w in range(ITERS):
                term = coords[w] * load(w, start)
                strip = term if strip is None else strip + term
            target[pl.ds(start, 8), :] = strip
            return 0

        lax.fori_loop(0, height // 8, body, 0, unroll=height // 8)

    with jax.named_scope("blend"):
        for t in range(tiles):
            combine(lambda w, start: vec[w, t, pl.ds(start + TOP, 8), :], blend.at[t], rows)
            leave(blend.at[t], blend_out.at[:, pl.ds(t * LANES, LANES)])
    tall = mid.shape[1]
    with jax.named_scope("mid"):
        for q in range(mid.shape[0]):
            combine(lambda w, start: mids[w, q, pl.ds(start, 8), :], mid.at[q], tall)
            leave(mid.at[q], mid_out.at[:, pl.ds(q * LANES, LANES)])
    with jax.named_scope("coarse"):
        pool2 = pool_matrix(2)
        for q in range(coarse.shape[0]):
            coarse[q] = pooled(
                lambda tile, line: mid[2 * q + tile, pl.ds(line, tall // 2, stride=2), :], 2, pool2)
            leave(coarse.at[q], coarse_out.at[:, pl.ds(q * LANES, LANES)])
    with jax.named_scope("fine"):
        for q in range(tiles // 2):
            combine(lambda w, start: fines[w, q, pl.ds(start, 8), :], fine.at[q], rows // 2)
            leave(fine.at[q], fine_out.at[:, pl.ds(q * LANES, LANES)])
    with jax.named_scope("wait_out"):
        for copy in started:
            copy.wait()


def per_device(n_row, n_col, sources, labels):
    kinds, rows, cols = sources.shape
    n = n_row * n_col
    tiles = cols // LANES
    tall = rows + 2 * TOP
    n_pack = HALO * (kinds + 1)
    f32 = jnp.float32
    vmem = pl.BlockSpec(memory_space=pltpu.VMEM)
    hbm = pl.BlockSpec(memory_space=pltpu.HBM)
    mid_rows, coarse_rows = n_row * rows // 4, n_row * rows // 8
    chips = n_row // 2
    dma = pltpu.SemaphoreType.DMA
    vec, fines, mids, coords = pl.pallas_call(
        functools.partial(gather_kernel, n_row, n_col, rows, cols, kinds),
        out_shape=(
            jax.ShapeDtypeStruct((ITERS, tiles + 1, tall, LANES), f32),
            jax.ShapeDtypeStruct((ITERS, tiles // 2, rows // 2, LANES), f32),
            jax.ShapeDtypeStruct((ITERS, tiles // 4, mid_rows, LANES), f32),
            jax.ShapeDtypeStruct((ITERS, 8, LANES), f32),
        ),
        in_specs=[hbm] * 2,
        out_specs=(vmem,) * 4,
        scratch_shapes=[
            pltpu.VMEM((kinds, tiles + 1, tall, LANES), f32),
            pltpu.VMEM((tiles + 1, tall, LANES), jnp.int32),
            pltpu.VMEM((kinds, 2, 8, cols), f32),
            pltpu.VMEM((2, 8, cols), jnp.int32),
            pltpu.VMEM((2, tiles, n_pack, LANES), f32),
            pltpu.VMEM((2, n_pack, rows), f32),
            pltpu.VMEM((2, tiles, n_pack, LANES), f32),
            pltpu.VMEM((2, n_pack, rows), f32),
            pltpu.VMEM((2, 2, n_pack, LANES), f32),
            pltpu.VMEM((2 * ITERS, 8, LANES), f32),
            pltpu.VMEM((n, 1, LANES), f32),
            dma((kinds + 1, tiles + 2)),
            dma((8,)),
            dma((8,)),
            dma,
            dma,
            dma((ITERS, chips)),
            dma((ITERS, chips)),
            dma((ITERS, chips)),
            dma((ITERS, chips)),
        ],
        compiler_params=pltpu.CompilerParams(
            collective_id=0, has_side_effects=True, vmem_limit_bytes=24 * 2**20),
    )(
        pltpu.with_memory_space_constraint(sources, pltpu.HBM),
        pltpu.with_memory_space_constraint(labels, pltpu.HBM),
    )
    return pl.pallas_call(
        functools.partial(finish_kernel, rows, cols),
        out_shape=(
            jax.ShapeDtypeStruct((rows, cols), f32),
            jax.ShapeDtypeStruct((rows // 2, cols // 2), f32),
            jax.ShapeDtypeStruct((mid_rows, cols // 4), f32),
            jax.ShapeDtypeStruct((coarse_rows, cols // 8), f32),
        ),
        in_specs=[vmem] * 4,
        out_specs=(hbm,) * 4,
        scratch_shapes=[
            pltpu.VMEM((tiles, rows, LANES), f32),
            pltpu.VMEM((tiles // 2, rows // 2, LANES), f32),
            pltpu.VMEM((tiles // 4, mid_rows, LANES), f32),
            pltpu.VMEM((tiles // 8, coarse_rows, LANES), f32),
            dma((tiles + tiles // 2 + tiles // 4 + tiles // 8,)),
        ],
        compiler_params=pltpu.CompilerParams(vmem_limit_bytes=24 * 2**20),
    )(vec, fines, mids, coords)


def solution(mesh):
    sizes = dict(mesh.shape)
    return jax.shard_map(
        functools.partial(per_device, sizes["row"], sizes["col"]),
        mesh=mesh,
        in_specs=(P(None, "row", "col"), P("row", "col")),
        out_specs=(P("row", "col"), P("row", "col"), P(None, "col"), P(None, "col")),
        check_vma=False,
    )
```

time: 25 us -> 21.8 us (0.87)
  Pallas kernels: 24.2 us -> 21 us
    pallas_call x1, Pallas kernels: 22.7 us -> 19.8 us  [per_device(): pl.pallas_call(functools.partial(gather_kernel, n_row, n_col, rows, cols,...]
    pallas_call x1, Pallas kernels: 1.44 us -> 1.15 us  [per_device(): pl.pallas_call(functools.partial(finish_kernel, rows, cols), out_shape=(j...]
where the time goes in v1:
time: 21.8 us; the launch traced here: 21.6 us
  Pallas kernels  21 us (96%)
  between operations  0.64 us (3%)
    pallas_call x1, Pallas kernels, per_device(): pl.pallas_call(functools.partial(gather_kernel, n_row, n_col, rows, cols,...  19.8 us
    pallas_call x1, Pallas kernels, per_device(): pl.pallas_call(functools.partial(finish_kernel, rows, cols), out_shape=(j...  1.15 us

profile of v1, /device:TPU:0, one launch (start us, length us, event | category | flops | bytes accessed | tf_op | source)
XLA Modules:
  0.0 21.6 jit_solution(18152099516280593545)
XLA Ops:
  0.6 19.8 %shard_map.57 = (f32[3,9,144,128]{3,2,1,0:T(8,128)S(1)}, f32[3,4,64,128]{3,2,1,0:T(8,128)S(1)}, f32[3,2,256,128]{3,2,1,0:T(8,128)S(1)}, f32[3,8,128]{2,1,0:T(8,128)S(1)}) custom-call(f32[3,128,1024]{2,1,0:T(8,128)} %src_hbm.1, s32[128,1024]{1,0:T(8,128)} %lab_hbm.1), custom_call_target="tpu_custom_call" | custom-call | tf_op jit(solution)/shard_map/pallas_call | solution.py:556
  20.5 1.2 %shard_map.58 = (f32[128,1024]{1,0:T(8,128)}, f32[64,512]{1,0:T(8,128)}, f32[256,256]{1,0:T(8,128)}, f32[128,128]{1,0:T(8,128)}) custom-call(f32[3,9,144,128]{3,2,1,0:T(8,128)S(1)} %get-tuple-element.8.vec, f32[3,4,64,128]{3,2,1,0:T(8,128)S(1)} %get-tuple-element.9.fines, f32[3,2,256,128]{3,2,1,0:T(8,128)S(1)} %get-tuple-element.10.mids, ...), custom_call_target="tpu_custom_call" | custom-call | tf_op jit(solution)/shard_map/pallas_call | solution.py:594

commit v2 on v1

--- a/solution.py
+++ b/solution.py
@@ -94,13 +94,13 @@
 
 
 def split_dot(values, pool):
-    total = None
+    pieces = []
     for _ in range(3):
-        piece = values.astype(jnp.bfloat16)
-        values = values - piece.astype(jnp.float32)
-        part = jnp.dot(piece, pool, preferred_element_type=jnp.float32)
-        total = part if total is None else total + part
-    return total
+        pieces.append(values.astype(jnp.bfloat16))
+        values = values - pieces[-1].astype(jnp.float32)
+    parts = jnp.dot(jnp.concatenate(pieces, axis=0), pool, preferred_element_type=jnp.float32)
+    size = values.shape[0]
+    return (parts[0:size] + parts[size:2 * size]) + parts[2 * size:]
 
 
 def pooled(load, stride, pool):
@@ -123,7 +123,8 @@
     n_row, n_col, rows, cols, kinds,
     src_hbm, lab_hbm, vec, fines, mids, coord_ref,
     src, lab, edge, edge_lab, pack_r, pack_c, got_r, got_c, got_d, part, moment,
-    load_sem, send_sem, recv_sem, mom_send, mom_recv, mid_send, mid_recv, fwd_send, fwd_recv,
+    band, patch, load_sem, send_sem, recv_sem, chain, mom_send, mom_recv, mid_send, near_recv, far_recv,
+    fwd_send, fwd_recv, patch_send, patch_recv,
 ):
     tiles = cols // LANES
     side_tile = tiles
@@ -134,52 +135,65 @@
     me = row * n_col + col
     f32 = jnp.float32
 
-    def plane_load(k, t):
+    first_row, last_row = row == 0, row == n_row - 1
+    first_col, last_col = col == 0, col == n_col - 1
+    there = {
+        (dr, dc): functools.reduce(jnp.logical_and, [
+            jnp.logical_not(edge) for step, edge in (
+                (dr < 0, first_row), (dr > 0, last_row), (dc < 0, first_col), (dc > 0, last_col))
+            if step])
+        for dr, dc in SIDES
+    }
+
+    def other_row(step):
+        return jnp.where(step >= row, step + 1, step)
+
+    def for_other_rows(act):
+        def body(step, _):
+            act(other_row(step))
+            return 0
+
+        lax.fori_loop(0, n_row - 1, body, 0)
+
+    barrier = pltpu.get_barrier_semaphore()
+
+    def greet(r, c):
+        pl.semaphore_signal(barrier, inc=1, device_id=(r, c), device_id_type=MESH)
+
+    greeters = n_row - 1
+    for dr, dc in SIDES:
+        if dc:
+            pl.when(there[dr, dc])(functools.partial(
+                greet, jnp.clip(row + dr, 0, n_row - 1), jnp.clip(col + dc, 0, n_col - 1)))
+            greeters = greeters + jnp.where(there[dr, dc], 1, 0)
+    def plane_load(k, t, wave):
         lanes = pl.ds(t * LANES, LANES)
         if k < kinds:
             return pltpu.make_async_copy(
-                src_hbm.at[k, :, lanes], src.at[k, t, body_rows], load_sem.at[k, t])
-        return pltpu.make_async_copy(lab_hbm.at[:, lanes], lab.at[t, body_rows], load_sem.at[k, t])
+                src_hbm.at[k, :, lanes], src.at[k, t, body_rows], load_sem.at[2 * wave])
+        return pltpu.make_async_copy(
+            lab_hbm.at[:, lanes], lab.at[t, body_rows], load_sem.at[2 * wave + 1])
 
     def edge_load(k, side):
         here = pl.ds(0 if side == 0 else rows - 8, 8)
         if k < kinds:
-            return pltpu.make_async_copy(
-                src_hbm.at[k, here], edge.at[k, side], load_sem.at[k, tiles + side])
-        return pltpu.make_async_copy(lab_hbm.at[here], edge_lab.at[side], load_sem.at[k, tiles + side])
-
-    first_loads = [plane_load(k, t) for k in range(kinds + 1) for t in (0, tiles - 1)]
-    first_loads += [edge_load(k, side) for k in range(kinds + 1) for side in range(2)]
-    later_loads = [plane_load(k, t) for t in range(1, tiles - 1) for k in range(kinds + 1)]
-    for load in first_loads:
-        load.start()
-
-    barrier = pltpu.get_barrier_semaphore()
-
-    columns = [col]
-    for _ in range(n_col - 1):
-        columns.append(jnp.where(columns[-1] + 1 == n_col, 0, columns[-1] + 1))
-
-    def for_all_others(act):
-        for c in columns[1:]:
-            act(row, c)
-
-        def body(step, _):
-            r = row + step
-            r = jnp.where(r >= n_row, r - n_row, r)
-            for c in columns:
-                act(r, c)
-            return 0
-
-        lax.fori_loop(1, n_row, body, 0)
-
-    for_all_others(lambda r, c: pl.semaphore_signal(
-        barrier, inc=1, device_id=(r, c), device_id_type=MESH))
-    for load in later_loads:
-        load.start()
-
-    first_row, last_row = row == 0, row == n_row - 1
-    first_col, last_col = col == 0, col == n_col - 1
+            return pltpu.make_async_copy(src_hbm.at[k, here], edge.at[k, side], load_sem.at[4])
+        return pltpu.make_async_copy(lab_hbm.at[here], edge_lab.at[side], load_sem.at[5])
+
+    def wait_bytes(ref, sem):
+        pltpu.make_async_copy(ref, ref, sem).wait()
+
+    for k in range(kinds + 1):
+        for side in range(2):
+            edge_load(k, side).start()
+    for k in range(kinds + 1):
+        for t in (0, tiles - 1):
+            plane_load(k, t, 0).start()
+    for_other_rows(lambda r: greet(r, col))
+    for t in range(1, tiles - 1):
+        for k in range(kinds + 1):
+            plane_load(k, t, 1).start()
+
     pad = jnp.zeros((tiles + 1, 8, LANES), f32)
     for start in (0, TOP + rows):
         for k in range(kinds):
@@ -190,8 +204,10 @@
 
     n_pack = HALO * (kinds + 1)
     with jax.named_scope("wait_first"):
-        for load in first_loads:
-            load.wait()
+        wait_bytes(edge, load_sem.at[4])
+        wait_bytes(edge_lab, load_sem.at[5])
+        wait_bytes(src.at[:, pl.ds(0, 2), body_rows], load_sem.at[0])
+        wait_bytes(lab.at[pl.ds(0, 2), body_rows], load_sem.at[1])
     with jax.named_scope("pack"):
         for k in range(kinds + 1):
             at = pl.ds(HALO * k, HALO)
@@ -217,7 +233,7 @@
             pack_c[1, at, :] = turned[LANES - HALO:LANES]
 
     with jax.named_scope("barrier"):
-        pl.semaphore_wait(barrier, n - 1)
+        pl.semaphore_wait(barrier, greeters)
 
     sends = []
     for i, (dr, dc) in enumerate(SIDES):
@@ -229,10 +245,6 @@
         else:
             source = pack_r.at[mine_r, 0 if dc < 0 else tiles - 1]
             target, here = got_d.at[1 - mine_r, 1 - mine_c], got_d.at[mine_r, mine_c]
-        there = jnp.logical_and(
-            jnp.logical_and(row + dr >= 0, row + dr < n_row),
-            jnp.logical_and(col + dc >= 0, col + dc < n_col),
-        )
         opposite = SIDES.index((-dr, -dc))
         device = (
             jnp.clip(row + dr, 0, n_row - 1),
@@ -246,12 +258,29 @@
             src_ref=source, dst_ref=here, send_sem=send_sem.at[i],
             recv_sem=recv_sem.at[i], device_id=device, device_id_type=MESH,
         )
-        sends.append((there, copy, back))
-        pl.when(there)(copy.start)
+        sends.append((there[dr, dc], copy, back))
+        pl.when(there[dr, dc])(copy.start)
+
+    def pass_on(dc):
+        pl.semaphore_signal(
+            chain.at[0 if dc > 0 else 1], inc=1,
+            device_id=(row, jnp.clip(col + dc, 0, n_col - 1)), device_id_type=MESH)
+
+    def hear(dc):
+        pl.semaphore_wait(chain.at[0 if dc > 0 else 1], 1)
+
+    def relay(dc):
+        hear(dc)
+        pass_on(dc)
+
+    inner_col = jnp.logical_and(there[0, 1], there[0, -1])
+    upper_half = 2 * col >= n_col
+    pl.when(jnp.logical_and(first_col, there[0, 1]))(lambda: pass_on(1))
+    pl.when(jnp.logical_and(last_col, there[0, -1]))(lambda: pass_on(-1))
 
     with jax.named_scope("wait_later"):
-        for load in later_loads:
-            load.wait()
+        wait_bytes(src.at[:, pl.ds(1, tiles - 2), body_rows], load_sem.at[2])
+        wait_bytes(lab.at[pl.ds(1, tiles - 2), body_rows], load_sem.at[3])
     groups = rows // 8
     lane_r = lane_of((tiles, 8, LANES))
     lane_t = lane_of((8, LANES))
@@ -278,6 +307,54 @@
         for which in range(1, ITERS):
             whole_loop(groups, lambda i: save(
                 which, main, TOP + 8 * i, applied(which - 1, main, TOP + 8 * i, beside_ring)))
+
+    chips = n_row // 2
+    core = lax.rem(row, 2)
+    chip = lax.div(row, 2)
+    partner = row + 1 - 2 * core
+    quad = rows // 4
+    pool4, pool2 = pool_matrix(4), pool_matrix(2)
+
+    def some(w, count):
+        return mids.at[w, :, pl.ds(0, count * quad)]
+
+    def hand(w, owner, target, send, recv):
+        block = mids.at[w, :, pl.ds(pl.multiple_of(owner * quad, 8), quad)]
+        pltpu.make_async_remote_copy(
+            src_ref=block, dst_ref=block, send_sem=send, recv_sem=recv,
+            device_id=(target, col), device_id_type=MESH).start()
+
+    def same_core(q):
+        return 2 * q + core
+
+    def to_partner(w, owner):
+        hand(w, owner, partner, fwd_send, fwd_recv)
+
+    if chips == 4:
+        beside = [chip + 1 - 2 * lax.rem(chip, 2), chip + 2 - 4 * lax.div(chip, 2)]
+        across = 3 - chip
+        via = same_core(jnp.where(core == 0, beside[0], beside[1]))
+        onward = same_core(jnp.where(core == 0, beside[1], beside[0]))
+        near = [same_core(q) for q in beside]
+    else:
+        near = []
+        for step in range(1, chips):
+            q = chip + step
+            near.append(same_core(jnp.where(q >= chips, q - chips, q)))
+
+    with jax.named_scope("early"):
+        for w in range(ITERS):
+            own = pooled(
+                lambda tile, line: jnp.concatenate([
+                    vec[w, 4 * q + tile, pl.ds(TOP + line, quad, stride=4), :]
+                    for q in range(tiles // 4)], axis=0),
+                4, pool4)
+            for q in range(tiles // 4):
+                mids[w, q, pl.ds(pl.multiple_of(row * quad, 8), quad), :] = own[
+                    q * quad:(q + 1) * quad]
+            for target in near:
+                hand(w, row, target, mid_send, near_recv.at[w])
+            to_partner(w, row)
 
     def products(tile, start, beside, keep):
         powers = [lines(vec, (w, tile), start) for w in range(ITERS)]
@@ -321,9 +398,13 @@
                 lab[side_tile, body_rows, :] = jnp.where(
                     wide_lane < LANES // 2, pltpu.roll(first, 2 * HALO, axis=1), last)
 
+    with jax.named_scope("relay"):
+        pl.when(inner_col)(lambda: relay(1))
+        pl.when(jnp.logical_and(inner_col, upper_half))(lambda: relay(-1))
+
     with jax.named_scope("wait_halo"):
-        for there, copy, back in sends:
-            pl.when(there)(back.wait_recv)
+        for exists, copy, back in sends:
+            pl.when(exists)(back.wait_recv)
 
     with jax.named_scope("unpack"):
         for k in range(kinds + 1):
@@ -398,58 +479,123 @@
         moment[me] = mine
 
     with jax.named_scope("send_moments"):
-        for_all_others(lambda r, c: pltpu.make_async_remote_copy(
-            src_ref=moment.at[me], dst_ref=moment.at[me], send_sem=mom_send, recv_sem=mom_recv,
-            device_id=(r, c), device_id_type=MESH).start())
-
-    chips = n_row // 2
-    partner = row + 1 - 2 * lax.rem(row, 2)
-    quad = rows // 4
-    pool4, pool2 = pool_matrix(4), pool_matrix(2)
-
-    def block(w, owner):
-        return mids.at[w, :, pl.ds(pl.multiple_of(owner * quad, 8), quad)]
-
-    def peer(step):
-        other = row + 2 * step
-        return jnp.where(other >= n_row, other - n_row, other)
-
-    def hand(w, owner, target, send, recv):
-        return pltpu.make_async_remote_copy(
-            src_ref=block(w, owner), dst_ref=block(w, owner), send_sem=send, recv_sem=recv,
-            device_id=(target, col), device_id_type=MESH)
-
-    hops = []
-    with jax.named_scope("mids"):
+        pl.when(jnp.logical_and(last_col, there[0, -1]))(lambda: hear(1))
+
+        def tell(r, c):
+            pltpu.make_async_remote_copy(
+                src_ref=moment.at[me], dst_ref=moment.at[me], send_sem=mom_send, recv_sem=mom_recv,
+                device_id=(r, c), device_id_type=MESH).start()
+
+        def tell_block(c):
+            def body(r, _):
+                tell(r, c)
+                return 0
+
+            lax.fori_loop(0, n_row, body, 0)
+
+        for c in range(n_col - 1):
+            pl.when(c < col)(functools.partial(tell_block, c))
+        for_other_rows(lambda r: tell(r, col))
+        pl.when(jnp.logical_and(inner_col, jnp.logical_not(upper_half)))(lambda: relay(-1))
+
+    def tell_rest():
+        pl.when(first_col)(lambda: hear(-1))
+        for c in range(1, n_col):
+            pl.when(c > col)(functools.partial(tell_block, c))
+
+    with jax.named_scope("tell_inner"):
+        pl.when(inner_col)(tell_rest)
+
+    ends_of = ((0, TOP), (quad - 1, TOP + rows - 4))
+    lines_of = [(w, e, q) for w in range(ITERS) for e in range(2) for q in range(tiles // 4)]
+    with jax.named_scope("patch"):
+        for at, (w, e, q) in enumerate(lines_of):
+            for i in range(4):
+                four = vec[w, 4 * q + i, pl.ds(ends_of[e][1], 4), :]
+                band[i, at:at + 1, :] = jnp.sum(four, axis=0, keepdims=True)
+        wide = jnp.concatenate([band[i] for i in range(4)], axis=1)
+        patch[row, 0:wide.shape[0], :] = split_dot(wide, pool4)
+        odd = lax.rem(row, 2) == 1
+        row_lane = lane_of((1, rows))
+        for w in range(ITERS):
+            flat = vec[w, side_tile, pl.ds(TOP, quad, stride=4), :]
+            for line in range(1, 4):
+                flat = flat + vec[w, side_tile, pl.ds(TOP + line, quad, stride=4), :]
+            even_part, odd_part = jnp.where(odd, 0.0, flat), jnp.where(odd, flat, 0.0)
+            turned = jnp.transpose(jnp.concatenate([even_part, odd_part] * 2, axis=0))
+            left = jnp.sum(turned[2 * HALO:3 * HALO], axis=0, keepdims=True)
+            right = jnp.sum(turned[LANES - HALO:], axis=0, keepdims=True)
+            at = len(lines_of) + w
+            patch[row, at:at + 1, :] = jnp.where(row_lane < 2 * quad, left, right) * (1.0 / 16)
+        for_other_rows(lambda r: pltpu.make_async_remote_copy(
+            src_ref=patch.at[row], dst_ref=patch.at[row], send_sem=patch_send,
+            recv_sem=patch_recv, device_id=(r, col), device_id_type=MESH).start())
+
+    with jax.named_scope("near"):
+        for w in range(ITERS):
+            wait_bytes(some(w, len(near)), near_recv.at[w])
+            if chips == 4:
+                hand(w, via, onward, mid_send, far_recv.at[w])
+            for owner in near:
+                to_partner(w, owner)
+    with jax.named_scope("merge"):
         for w in range(ITERS):
             side = vec[w, side_tile, body_rows]
             vec[w, 0, body_rows, :] = jnp.where(
                 wide_lane < HALO, pltpu.roll(side, LANES - 2 * HALO, axis=1), vec[w, 0, body_rows])
             vec[w, tiles - 1, body_rows, :] = jnp.where(
                 wide_lane >= LANES - HALO, side, vec[w, tiles - 1, body_rows])
-            for q in range(tiles // 4):
-                mids[w, q, pl.ds(pl.multiple_of(row * quad, 8), quad), :] = pooled(
-                    lambda tile, line: vec[w, 4 * q + tile, pl.ds(TOP + line, quad, stride=4), :],
-                    4, pool4)
-            here = [
-                hand(w, row, peer(step), mid_send.at[w, step], mid_recv.at[w, step])
-                for step in range(1, chips)
-            ]
-            here.append(hand(w, row, partner, mid_send.at[w, 0], mid_recv.at[w, 0]))
-            for hop in here:
-                hop.start()
-            hops += here
+
     with jax.named_scope("fines"):
+        half = rows // 2
         for w in range(ITERS):
+            own = pooled(
+                lambda tile, line: jnp.concatenate([
+                    vec[w, 2 * q + tile, pl.ds(TOP + line, half, stride=2), :]
+                    for q in range(tiles // 2)], axis=0),
+                2, pool2)
             for q in range(tiles // 2):
-                fines[w, q] = pooled(
-                    lambda tile, line: vec[
-                        w, 2 * q + tile, pl.ds(TOP + line, rows // 2, stride=2), :],
-                    2, pool2)
+                fines[w, q] = own[q * half:(q + 1) * half]
+
+    if chips == 4:
+        with jax.named_scope("far"):
+            for w in range(ITERS):
+                wait_bytes(some(w, 1), far_recv.at[w])
+                to_partner(w, same_core(across))
+
+    with jax.named_scope("tell_first"):
+        pl.when(jnp.logical_and(first_col, there[0, 1]))(tell_rest)
+
+    every_core = mids.at[:, :, pl.ds(0, chips * quad)]
+    with jax.named_scope("wait_forwards"):
+        wait_bytes(mids.at[:, :, pl.ds(0, (chips - 1) * quad)], mid_send)
+        wait_bytes(every_core, fwd_send)
+        wait_bytes(every_core, fwd_recv)
+    with jax.named_scope("wait_patch"):
+        patches = patch.at[pl.ds(0, n_row - 1)]
+        wait_bytes(patches, patch_recv)
+    with jax.named_scope("apply"):
+        for owner in range(n_row):
+            for at, (w, e, q) in enumerate(lines_of):
+                mids[w, q, pl.ds(owner * quad + ends_of[e][0], 1), :] = patch[
+                    owner, at:at + 1, :]
+        tall_lane = lane_of((2 * quad, LANES))
+        for pair in range(n_row // 2):
+            there_rows = pl.ds(2 * pair * quad, 2 * quad)
+            for w in range(ITERS):
+                at = len(lines_of) + w
+                both = patch[2 * pair, at:at + 1, :] + patch[2 * pair + 1, at:at + 1, :]
+                turned = jnp.transpose(jnp.broadcast_to(both, (8, LANES)))
+                for q, lane, lines_here in (
+                        (0, 0, turned[0:2 * quad]),
+                        (tiles // 4 - 1, LANES - 1, turned[2 * quad:])):
+                    value = jnp.broadcast_to(lines_here[:, 0:1], (2 * quad, LANES))
+                    mids[w, q, there_rows, :] = jnp.where(
+                        tall_lane == lane, value, mids[w, q, there_rows, :])
 
     with jax.named_scope("wait_moments"):
         everyone = moment.at[pl.ds(0, n - 1)]
-        pltpu.make_async_copy(everyone, everyone, mom_recv).wait()
+        wait_bytes(everyone, mom_recv)
     with jax.named_scope("coefs"):
         total = jnp.sum(moment[...], axis=0)
         moments = [
@@ -459,36 +605,11 @@
         for w, c in enumerate(coefficients(moments)):
             coord_ref[w] = jnp.broadcast_to(0.25 ** w * c, (8, LANES))
 
-    def source_of(step):
-        other = row - 2 * step
-        return jnp.where(other < 0, other + n_row, other)
-
-    def other_core(owner):
-        return owner + 1 - 2 * lax.rem(owner, 2)
-
-    with jax.named_scope("forwards"):
-        forwards = []
-        for w in range(ITERS):
-            for step in range(1, chips):
-                owner = source_of(step)
-                hand(w, owner, partner, mid_send.at[w, step], mid_recv.at[w, step]).wait_recv()
-                forward = hand(w, owner, partner, fwd_send.at[w, step], fwd_recv.at[w, step])
-                forward.start()
-                forwards.append(forward)
-    with jax.named_scope("wait_forwards"):
-        for w in range(ITERS):
-            hand(w, partner, partner, mid_send.at[w, 0], mid_recv.at[w, 0]).wait_recv()
-            for step in range(1, chips):
-                hand(w, other_core(source_of(step)), partner,
-                     fwd_send.at[w, step], fwd_recv.at[w, step]).wait_recv()
     with jax.named_scope("wait_sends"):
-        for hop in hops:
-            hop.wait_send()
-        for forward in forwards:
-            forward.wait_send()
-        for there, copy, back in sends:
-            pl.when(there)(copy.wait_send)
-        pltpu.make_async_copy(everyone, everyone, mom_send).wait()
+        for exists, copy, back in sends:
+            pl.when(exists)(copy.wait_send)
+        wait_bytes(everyone, mom_send)
+        wait_bytes(patches, patch_send)
 
 
 def finish_kernel(
@@ -496,12 +617,10 @@
     blend, fine, mid, coarse, out_sem,
 ):
     tiles = cols // LANES
-    started = []
-
-    def leave(source, target):
-        copy = pltpu.make_async_copy(source, target, out_sem.at[len(started)])
-        copy.start()
-        started.append(copy)
+
+    def leave(which, source, target, q):
+        pltpu.make_async_copy(
+            source.at[q], target.at[:, pl.ds(q * LANES, LANES)], out_sem.at[which]).start()
 
     def combine(load, target, height):
         coords = [coord_ref[w] for w in range(ITERS)]
@@ -517,28 +636,28 @@
 
         lax.fori_loop(0, height // 8, body, 0, unroll=height // 8)
 
-    with jax.named_scope("blend"):
-        for t in range(tiles):
-            combine(lambda w, start: vec[w, t, pl.ds(start + TOP, 8), :], blend.at[t], rows)
-            leave(blend.at[t], blend_out.at[:, pl.ds(t * LANES, LANES)])
     tall = mid.shape[1]
     with jax.named_scope("mid"):
         for q in range(mid.shape[0]):
             combine(lambda w, start: mids[w, q, pl.ds(start, 8), :], mid.at[q], tall)
-            leave(mid.at[q], mid_out.at[:, pl.ds(q * LANES, LANES)])
+            leave(1, mid, mid_out, q)
+    with jax.named_scope("blend"):
+        for t in range(tiles):
+            combine(lambda w, start: vec[w, t, pl.ds(start + TOP, 8), :], blend.at[t], rows)
+            leave(0, blend, blend_out, t)
+    with jax.named_scope("fine"):
+        for q in range(tiles // 2):
+            combine(lambda w, start: fines[w, q, pl.ds(start, 8), :], fine.at[q], rows // 2)
+            leave(2, fine, fine_out, q)
     with jax.named_scope("coarse"):
         pool2 = pool_matrix(2)
         for q in range(coarse.shape[0]):
             coarse[q] = pooled(
                 lambda tile, line: mid[2 * q + tile, pl.ds(line, tall // 2, stride=2), :], 2, pool2)
-            leave(coarse.at[q], coarse_out.at[:, pl.ds(q * LANES, LANES)])
-    with jax.named_scope("fine"):
-        for q in range(tiles // 2):
-            combine(lambda w, start: fines[w, q, pl.ds(start, 8), :], fine.at[q], rows // 2)
-            leave(fine.at[q], fine_out.at[:, pl.ds(q * LANES, LANES)])
+            leave(3, coarse, coarse_out, q)
     with jax.named_scope("wait_out"):
-        for copy in started:
-            copy.wait()
+        for which, ref in enumerate((blend, mid, fine, coarse)):
+            pltpu.make_async_copy(ref, ref, out_sem.at[which]).wait()
 
 
 def per_device(n_row, n_col, sources, labels):
@@ -575,15 +694,21 @@
             pltpu.VMEM((2, 2, n_pack, LANES), f32),
             pltpu.VMEM((2 * ITERS, 8, LANES), f32),
             pltpu.VMEM((n, 1, LANES), f32),
-            dma((kinds + 1, tiles + 2)),
+            pltpu.VMEM((4, ITERS * (tiles // 2), LANES), f32),
+            pltpu.VMEM((n_row, ITERS * (tiles // 2) + 4, LANES), f32),
+            dma((6,)),
             dma((8,)),
             dma((8,)),
+            pltpu.SemaphoreType.REGULAR((2,)),
             dma,
             dma,
-            dma((ITERS, chips)),
-            dma((ITERS, chips)),
-            dma((ITERS, chips)),
-            dma((ITERS, chips)),
+            dma,
+            dma((ITERS,)),
+            dma((ITERS,)),
+            dma,
+            dma,
+            dma,
+            dma,
         ],
         compiler_params=pltpu.CompilerParams(
             collective_id=0, has_side_effects=True, vmem_limit_bytes=24 * 2**20),
@@ -606,7 +731,7 @@
             pltpu.VMEM((tiles // 2, rows // 2, LANES), f32),
             pltpu.VMEM((tiles // 4, mid_rows, LANES), f32),
             pltpu.VMEM((tiles // 8, coarse_rows, LANES), f32),
-            dma((tiles + tiles // 2 + tiles // 4 + tiles // 8,)),
+            dma((4,)),
         ],
         compiler_params=pltpu.CompilerParams(vmem_limit_bytes=24 * 2**20),
     )(vec, fines, mids, coords)

time: 21.8 us -> 17.2 us (0.79)
  Pallas kernels: 21 us -> 16.4 us
    pallas_call x1, Pallas kernels: 19.8 us -> 15.4 us  [per_device(): pl.pallas_call(functools.partial(gather_kernel, n_row, n_col, rows, cols,...]
where the time goes in v2:
time: 17.2 us; the launch traced here: 17 us
  Pallas kernels  16.4 us (95%)
  between operations  0.64 us (4%)
    pallas_call x1, Pallas kernels, per_device(): pl.pallas_call(functools.partial(gather_kernel, n_row, n_col, rows, cols,...  15.4 us
    pallas_call x1, Pallas kernels, per_device(): pl.pallas_call(functools.partial(finish_kernel, rows, cols), out_shape=(j...  1.02 us

profile of v2, /device:TPU:0, one launch (start us, length us, event | category | flops | bytes accessed | tf_op | source)
XLA Modules:
  0.0 17.0 jit_solution(8001251554155161713)
XLA Ops:
  0.6 15.4 %shard_map.57 = (f32[3,9,144,128]{3,2,1,0:T(8,128)S(1)}, f32[3,4,64,128]{3,2,1,0:T(8,128)S(1)}, f32[3,2,256,128]{3,2,1,0:T(8,128)S(1)}, f32[3,8,128]{2,1,0:T(8,128)S(1)}) custom-call(f32[3,128,1024]{2,1,0:T(8,128)} %src_hbm.1, s32[128,1024]{1,0:T(8,128)} %lab_hbm.1), custom_call_target="tpu_custom_call" | custom-call | tf_op jit(solution)/shard_map/pallas_call | solution.py:675
  16.0 1.0 %shard_map.58 = (f32[128,1024]{1,0:T(8,128)}, f32[64,512]{1,0:T(8,128)}, f32[256,256]{1,0:T(8,128)}, f32[128,128]{1,0:T(8,128)}) custom-call(f32[3,9,144,128]{3,2,1,0:T(8,128)S(1)} %get-tuple-element.8.vec, f32[3,4,64,128]{3,2,1,0:T(8,128)S(1)} %get-tuple-element.9.fines, f32[3,2,256,128]{3,2,1,0:T(8,128)S(1)} %get-tuple-element.10.mids, ...), custom_call_target="tpu_custom_call" | custom-call | tf_op jit(solution)/shard_map/pallas_call | solution.py:719

commit v3 on v2

--- a/solution.py
+++ b/solution.py
@@ -8,6 +8,7 @@
 from jax.sharding import PartitionSpec as P
 
 ITERS = 3
+DIRECT = 3
 MESH = pl.DeviceIdType.MESH
 HALO = 4
 TOP = 8
@@ -53,6 +54,41 @@
         term = 4.0 * mid - neighbour_sum(src, (k, tile), start, mid, beside)
         total = term if total is None else jnp.where(here == k, term, total)
     return total
+
+
+def from_left(values):
+    lane = lane_of(values.shape)
+    moved = pltpu.roll(values, 1, axis=2)
+    return jnp.where(lane == 0, jnp.concatenate([moved[-1:], moved[:-1]], axis=0), moved)
+
+
+def from_right(values):
+    lane = lane_of(values.shape)
+    moved = pltpu.roll(values, LANES - 1, axis=2)
+    return jnp.where(lane == LANES - 1, jnp.concatenate([moved[1:], moved[:1]], axis=0), moved)
+
+
+def chosen(here, values):
+    total = values[-1]
+    for k in reversed(range(len(values) - 1)):
+        total = jnp.where(here == k, values[k], total)
+    return total
+
+
+def beside_chosen(src, lab, tile, start):
+    here = lines(lab, (tile,), start)
+    mids = [lines(src, (k, tile), start) for k in range(src.shape[0])]
+    return chosen(from_right(here), mids), chosen(from_left(here), mids)
+
+
+def right_side_ring(src, lab, tile, start, left, right):
+    here = lines(lab, (tile,), start)
+    crosses = [
+        4.0 * lines(src, (k, tile), start)
+        - (lines(src, (k, tile), start - 1) + lines(src, (k, tile), start + 1))
+        for k in range(src.shape[0])
+    ]
+    return chosen(here, crosses) - (from_left(left) + from_right(right))
 
 
 def quadratic(left, right, moments, shift):
@@ -122,8 +158,8 @@
 def gather_kernel(
     n_row, n_col, rows, cols, kinds,
     src_hbm, lab_hbm, vec, fines, mids, coord_ref,
-    src, lab, edge, edge_lab, pack_r, pack_c, got_r, got_c, got_d, part, moment,
-    band, patch, load_sem, send_sem, recv_sem, chain, mom_send, mom_recv, mid_send, near_recv, far_recv,
+    src, lab, edge, edge_lab, pack_up, pack_down, pack_c, pack_d, got_up, got_down, got_c, got_d,
+    part, moment, band, patch, sides, load_sem, send_sem, recv_sem, chain, mom_send, mom_recv, mid_send, near_recv, far_recv,
     fwd_send, fwd_recv, patch_send, patch_recv,
 ):
     tiles = cols // LANES
@@ -202,6 +238,11 @@
         for w in range(ITERS):
             vec[w, :, pl.ds(start, 8), :] = pad
 
+    def row_part(side, k, t):
+        depth = HALO - side
+        each = kinds * depth + depth - 1
+        return (depth if k < kinds else depth - 1), t * each + k * depth
+
     n_pack = HALO * (kinds + 1)
     with jax.named_scope("wait_first"):
         wait_bytes(edge, load_sem.at[4])
@@ -209,17 +250,25 @@
         wait_bytes(src.at[:, pl.ds(0, 2), body_rows], load_sem.at[0])
         wait_bytes(lab.at[pl.ds(0, 2), body_rows], load_sem.at[1])
     with jax.named_scope("pack"):
-        for k in range(kinds + 1):
-            at = pl.ds(HALO * k, HALO)
-            for side in range(2):
-                lines_here = pl.ds(0 if side == 0 else 8 - HALO, HALO)
+        for side in range(2):
+            for k in range(kinds + 1):
                 for t in range(tiles):
                     lanes = pl.ds(t * LANES, LANES)
+                    depth, at = row_part(side, k, t)
+                    lines_here = pl.ds(0 if side == 0 else 8 - depth, depth)
                     if k < kinds:
                         value = edge[k, side, lines_here, lanes]
                     else:
                         value = edge_lab[side, lines_here, lanes].astype(f32)
-                    pack_r[side, t, at, :] = value
+                    (pack_up if side == 0 else pack_down)[pl.ds(at, depth), :] = value
+                for end, t in enumerate((0, tiles - 1)):
+                    lanes = pl.ds(t * LANES, LANES)
+                    lines_here = pl.ds(0 if side == 0 else 8 - HALO, HALO)
+                    if k < kinds:
+                        value = edge[k, side, lines_here, lanes]
+                    else:
+                        value = edge_lab[side, lines_here, lanes].astype(f32)
+                    pack_d[side, end, pl.ds(HALO * k, HALO), :] = value
         wide_lane = lane_of((rows, LANES))
         for k in range(kinds + 1):
             if k < kinds:
@@ -239,11 +288,12 @@
     for i, (dr, dc) in enumerate(SIDES):
         mine_r, mine_c = (0 if dr < 0 else 1), (0 if dc < 0 else 1)
         if dc == 0:
-            source, target, here = pack_r.at[mine_r], got_r.at[1 - mine_r], got_r.at[mine_r]
+            source, target, here = (
+                (pack_up, got_up, got_down) if dr < 0 else (pack_down, got_down, got_up))
         elif dr == 0:
             source, target, here = pack_c.at[mine_c], got_c.at[1 - mine_c], got_c.at[mine_c]
         else:
-            source = pack_r.at[mine_r, 0 if dc < 0 else tiles - 1]
+            source = pack_d.at[mine_r, mine_c]
             target, here = got_d.at[1 - mine_r, 1 - mine_c], got_d.at[mine_r, mine_c]
         opposite = SIDES.index((-dr, -dc))
         device = (
@@ -301,12 +351,21 @@
         return neighbour_sum(vec, (which, tile), start, mid, beside)
 
     with jax.named_scope("main_b"):
+        def choose(i):
+            start = TOP + 8 * i
+            left, right = beside_chosen(src, lab, main, start)
+            save(1, main, start, left)
+            save(2, main, start, right)
+
+        whole_loop(groups, choose)
+        whole_loop(groups, lambda i: save(0, main, TOP + 8 * i, right_side_ring(
+            src, lab, main, TOP + 8 * i,
+            lines(vec, (1, main), TOP + 8 * i), lines(vec, (2, main), TOP + 8 * i))))
+
+    def inner(which):
         whole_loop(groups, lambda i: save(
-            0, main, TOP + 8 * i, right_side(src, lab, main, TOP + 8 * i, beside_ring)))
-    with jax.named_scope("main_v"):
-        for which in range(1, ITERS):
-            whole_loop(groups, lambda i: save(
-                which, main, TOP + 8 * i, applied(which - 1, main, TOP + 8 * i, beside_ring)))
+            which, main, TOP + 8 * i, applied(which - 1, main, TOP + 8 * i, beside_ring)))
+
 
     chips = n_row // 2
     core = lax.rem(row, 2)
@@ -342,25 +401,40 @@
             q = chip + step
             near.append(same_core(jnp.where(q >= chips, q - chips, q)))
 
-    with jax.named_scope("early"):
-        for w in range(ITERS):
-            own = pooled(
-                lambda tile, line: jnp.concatenate([
-                    vec[w, 4 * q + tile, pl.ds(TOP + line, quad, stride=4), :]
-                    for q in range(tiles // 4)], axis=0),
-                4, pool4)
-            for q in range(tiles // 4):
-                mids[w, q, pl.ds(pl.multiple_of(row * quad, 8), quad), :] = own[
-                    q * quad:(q + 1) * quad]
-            for target in near:
-                hand(w, row, target, mid_send, near_recv.at[w])
-            to_partner(w, row)
-
-    def products(tile, start, beside, keep):
+    def send_early(w):
+        own = pooled(
+            lambda tile, line: jnp.concatenate([
+                vec[w, 4 * q + tile, pl.ds(TOP + line, quad, stride=4), :]
+                for q in range(tiles // 4)], axis=0),
+            4, pool4)
+        for q in range(tiles // 4):
+            mids[w, q, pl.ds(pl.multiple_of(row * quad, 8), quad), :] = own[
+                q * quad:(q + 1) * quad]
+        for target in near:
+            hand(w, row, target, mid_send, near_recv.at[w])
+        if chips == 4 and w < DIRECT:
+            hand(w, row, same_core(across), mid_send, far_recv.at[w])
+        to_partner(w, row)
+
+    with jax.named_scope("main_v"):
+        for w in range(1, ITERS):
+            inner(w)
+            send_early(w - 1)
+        send_early(ITERS - 1)
+
+    def products(tile, start, right_of, keep):
         powers = [lines(vec, (w, tile), start) for w in range(ITERS)]
-        powers.append(neighbour_sum(vec, (ITERS - 1, tile), start, powers[-1], beside))
+        powers.append(lines(vec, (ITERS - 1, tile), start + 1) + right_of(powers[-1]))
         kept = [keep(p) for p in powers[:ITERS]]
         return [kept[i // 2] * powers[(i + 1) // 2] for i in range(2 * ITERS)]
+
+    def right_ring(mid):
+        right = pltpu.roll(mid, LANES - 1, axis=2)
+        return jnp.where(
+            lane_r == LANES - 1, jnp.concatenate([right[1:], right[:1]], axis=0), right)
+
+    def right_tile(mid):
+        return pltpu.roll(mid, LANES - 1, axis=1)
 
     def keep_main(p):
         edge_lane = lane_of((1, 8, LANES))
@@ -379,7 +453,7 @@
 
     with jax.named_scope("main_m"):
         def main_body(i, sums):
-            new = products(main, TOP + HALO + 8 * i, beside_ring, keep_main)
+            new = products(main, TOP + HALO + 8 * i, right_ring, keep_main)
             return tuple(s + fold(p) for s, p in zip(sums, new))
 
         zero8 = jnp.zeros((8, LANES), f32)
@@ -419,21 +493,28 @@
         corner_lane = lane_of((HALO, LANES))
         for side in range(2):
             missing = first_row if side == 0 else last_row
-            base = TOP - HALO if side == 0 else TOP + rows
+            got = got_down if side == 0 else got_up
             for k in range(kinds + 1):
+                wide = []
+                for t in range(tiles):
+                    depth, at = row_part(1 - side, k, t)
+                    wide.append(jnp.where(missing, 0.0, got[pl.ds(at, depth), :]))
+                shift = HALO - depth if side == 0 else 0
+                near_lines = slice(shift, shift + depth)
                 at = pl.ds(HALO * k, HALO)
-                wide = [jnp.where(missing, 0.0, got_r[side, t, at, :]) for t in range(tiles)]
-                right = jnp.where(missing | last_col, 0.0, got_d[side, 1, at, :])
-                left = jnp.where(missing | first_col, 0.0, got_d[side, 0, at, :])
+                right = jnp.where(missing | last_col, 0.0, got_d[side, 1, at, :])[near_lines]
+                left = jnp.where(missing | first_col, 0.0, got_d[side, 0, at, :])[near_lines]
+                corner_lane = lane_of((depth, LANES))
                 moved = pltpu.roll(
                     jnp.where(corner_lane >= LANES - HALO, left, wide[0]), 2 * HALO, axis=1)
                 own = jnp.where(corner_lane < LANES // 2, moved, wide[-1])
                 wide.append(jnp.where(corner_lane < HALO, right, own))
+                base = TOP - depth if side == 0 else TOP + rows
                 for t, value in enumerate(wide):
                     if k < kinds:
-                        src[k, t, pl.ds(base, HALO), :] = value
+                        src[k, t, pl.ds(base, depth), :] = value
                     else:
-                        lab[t, pl.ds(base, HALO), :] = value.astype(jnp.int32)
+                        lab[t, pl.ds(base, depth), :] = value.astype(jnp.int32)
 
     off_lane = ((lane_t < HALO) & last_col) | ((lane_t >= HALO) & (lane_t < 2 * HALO) & first_col)
     off_top = (line_t < HALO) & first_row
@@ -465,12 +546,12 @@
 
         def side_body(i, sums):
             new = products(
-                side_tile, TOP + 8 * i, beside_tile, lambda p: jnp.where(on_side, p, 0.0))
+                side_tile, TOP + 8 * i, right_tile, lambda p: jnp.where(on_side, p, 0.0))
             return tuple(s + p for s, p in zip(sums, new))
 
         sums = lax.fori_loop(0, groups, side_body, tuple(sums), unroll=groups)
         for (start, _), on in zip(ends, (line_t >= HALO, line_t < HALO)):
-            new = products(main, start, beside_ring, lambda p: jnp.where(on[None], keep_main(p), 0.0))
+            new = products(main, start, right_ring, lambda p: jnp.where(on[None], keep_main(p), 0.0))
             sums = [s + fold(p) for s, p in zip(sums, new)]
         lane1 = lane_of((1, LANES))
         mine = jnp.zeros((1, LANES), f32)
@@ -534,7 +615,7 @@
     with jax.named_scope("near"):
         for w in range(ITERS):
             wait_bytes(some(w, len(near)), near_recv.at[w])
-            if chips == 4:
+            if chips == 4 and w >= DIRECT:
                 hand(w, via, onward, mid_send, far_recv.at[w])
             for owner in near:
                 to_partner(w, owner)
@@ -557,41 +638,43 @@
             for q in range(tiles // 2):
                 fines[w, q] = own[q * half:(q + 1) * half]
 
+    with jax.named_scope("tell_first"):
+        pl.when(jnp.logical_and(first_col, there[0, 1]))(tell_rest)
+
     if chips == 4:
         with jax.named_scope("far"):
             for w in range(ITERS):
                 wait_bytes(some(w, 1), far_recv.at[w])
                 to_partner(w, same_core(across))
 
-    with jax.named_scope("tell_first"):
-        pl.when(jnp.logical_and(first_col, there[0, 1]))(tell_rest)
+    with jax.named_scope("wait_patch"):
+        patches = patch.at[pl.ds(0, n_row - 1)]
+        wait_bytes(patches, patch_recv)
+    with jax.named_scope("prepare"):
+        for pair in range(n_row // 2):
+            for w in range(ITERS):
+                at = len(lines_of) + w
+                both = patch[2 * pair, at:at + 1, :] + patch[2 * pair + 1, at:at + 1, :]
+                turned = jnp.transpose(jnp.broadcast_to(both, (8, LANES)))
+                for end in range(2):
+                    part_here = turned[2 * quad * end:2 * quad * (end + 1), 0:1]
+                    sides[w, end, pl.ds(2 * pair * quad, 2 * quad), :] = jnp.broadcast_to(
+                        part_here, (2 * quad, LANES))
 
     every_core = mids.at[:, :, pl.ds(0, chips * quad)]
     with jax.named_scope("wait_forwards"):
         wait_bytes(mids.at[:, :, pl.ds(0, (chips - 1) * quad)], mid_send)
         wait_bytes(every_core, fwd_send)
         wait_bytes(every_core, fwd_recv)
-    with jax.named_scope("wait_patch"):
-        patches = patch.at[pl.ds(0, n_row - 1)]
-        wait_bytes(patches, patch_recv)
     with jax.named_scope("apply"):
         for owner in range(n_row):
             for at, (w, e, q) in enumerate(lines_of):
                 mids[w, q, pl.ds(owner * quad + ends_of[e][0], 1), :] = patch[
                     owner, at:at + 1, :]
-        tall_lane = lane_of((2 * quad, LANES))
-        for pair in range(n_row // 2):
-            there_rows = pl.ds(2 * pair * quad, 2 * quad)
-            for w in range(ITERS):
-                at = len(lines_of) + w
-                both = patch[2 * pair, at:at + 1, :] + patch[2 * pair + 1, at:at + 1, :]
-                turned = jnp.transpose(jnp.broadcast_to(both, (8, LANES)))
-                for q, lane, lines_here in (
-                        (0, 0, turned[0:2 * quad]),
-                        (tiles // 4 - 1, LANES - 1, turned[2 * quad:])):
-                    value = jnp.broadcast_to(lines_here[:, 0:1], (2 * quad, LANES))
-                    mids[w, q, there_rows, :] = jnp.where(
-                        tall_lane == lane, value, mids[w, q, there_rows, :])
+        all_lane = lane_of((n_row * quad, LANES))
+        for w in range(ITERS):
+            for end, q, lane in ((0, 0, 0), (1, tiles // 4 - 1, LANES - 1)):
+                mids[w, q] = jnp.where(all_lane == lane, sides[w, end], mids[w, q])
 
     with jax.named_scope("wait_moments"):
         everyone = moment.at[pl.ds(0, n - 1)]
@@ -599,7 +682,8 @@
     with jax.named_scope("coefs"):
         total = jnp.sum(moment[...], axis=0)
         moments = [
-            0.25 ** i * jnp.sum(jnp.where(lane1 == i, total, 0.0), axis=1, keepdims=True)
+            (0.25 ** i * (1.0 if i < 2 * ITERS - 1 else 2.0))
+            * jnp.sum(jnp.where(lane1 == i, total, 0.0), axis=1, keepdims=True)
             for i in range(2 * ITERS)
         ]
         for w, c in enumerate(coefficients(moments)):
@@ -641,6 +725,11 @@
         for q in range(mid.shape[0]):
             combine(lambda w, start: mids[w, q, pl.ds(start, 8), :], mid.at[q], tall)
             leave(1, mid, mid_out, q)
+    with jax.named_scope("coarse"):
+        pool2 = pool_matrix(2)
+        for q in range(coarse.shape[0]):
+            coarse[q] = pooled(
+                lambda tile, line: mid[2 * q + tile, pl.ds(line, tall // 2, stride=2), :], 2, pool2)
     with jax.named_scope("blend"):
         for t in range(tiles):
             combine(lambda w, start: vec[w, t, pl.ds(start + TOP, 8), :], blend.at[t], rows)
@@ -649,11 +738,8 @@
         for q in range(tiles // 2):
             combine(lambda w, start: fines[w, q, pl.ds(start, 8), :], fine.at[q], rows // 2)
             leave(2, fine, fine_out, q)
-    with jax.named_scope("coarse"):
-        pool2 = pool_matrix(2)
+    with jax.named_scope("coarse_out"):
         for q in range(coarse.shape[0]):
-            coarse[q] = pooled(
-                lambda tile, line: mid[2 * q + tile, pl.ds(line, tall // 2, stride=2), :], 2, pool2)
             leave(3, coarse, coarse_out, q)
     with jax.named_scope("wait_out"):
         for which, ref in enumerate((blend, mid, fine, coarse)):
@@ -669,6 +755,7 @@
     f32 = jnp.float32
     vmem = pl.BlockSpec(memory_space=pltpu.VMEM)
     hbm = pl.BlockSpec(memory_space=pltpu.HBM)
+    up_lines, down_lines = ((kinds * d + d - 1) * tiles for d in (HALO, HALO - 1))
     mid_rows, coarse_rows = n_row * rows // 4, n_row * rows // 8
     chips = n_row // 2
     dma = pltpu.SemaphoreType.DMA
@@ -687,15 +774,19 @@
             pltpu.VMEM((tiles + 1, tall, LANES), jnp.int32),
             pltpu.VMEM((kinds, 2, 8, cols), f32),
             pltpu.VMEM((2, 8, cols), jnp.int32),
-            pltpu.VMEM((2, tiles, n_pack, LANES), f32),
+            pltpu.VMEM((up_lines, LANES), f32),
+            pltpu.VMEM((down_lines, LANES), f32),
             pltpu.VMEM((2, n_pack, rows), f32),
-            pltpu.VMEM((2, tiles, n_pack, LANES), f32),
+            pltpu.VMEM((2, 2, n_pack, LANES), f32),
+            pltpu.VMEM((up_lines, LANES), f32),
+            pltpu.VMEM((down_lines, LANES), f32),
             pltpu.VMEM((2, n_pack, rows), f32),
             pltpu.VMEM((2, 2, n_pack, LANES), f32),
             pltpu.VMEM((2 * ITERS, 8, LANES), f32),
             pltpu.VMEM((n, 1, LANES), f32),
             pltpu.VMEM((4, ITERS * (tiles // 2), LANES), f32),
             pltpu.VMEM((n_row, ITERS * (tiles // 2) + 4, LANES), f32),
+            pltpu.VMEM((ITERS, 2, mid_rows, LANES), f32),
             dma((6,)),
             dma((8,)),
             dma((8,)),

time: 17.2 us -> 16 us (0.930)
  Pallas kernels: 16.4 us -> 15.2 us
    pallas_call x1, Pallas kernels: 15.4 us -> 14.2 us  [per_device(): pl.pallas_call(functools.partial(gather_kernel, n_row, n_col, rows, cols,...]
where the time goes in v3:
time: 16 us; the launch traced here: 15.8 us
  Pallas kernels  15.2 us (95%)
  between operations  0.64 us (4%)
    pallas_call x1, Pallas kernels, per_device(): pl.pallas_call(functools.partial(gather_kernel, n_row, n_col, rows, cols,...  14.2 us
    pallas_call x1, Pallas kernels, per_device(): pl.pallas_call(functools.partial(finish_kernel, rows, cols), out_shape=(j...  1.02 us

profile of v3, /device:TPU:0, one launch (start us, length us, event | category | flops | bytes accessed | tf_op | source)
XLA Modules:
  0.0 15.8 jit_solution(2738401834028224485)
XLA Ops:
  0.6 14.2 %shard_map.57 = (f32[3,9,144,128]{3,2,1,0:T(8,128)S(1)}, f32[3,4,64,128]{3,2,1,0:T(8,128)S(1)}, f32[3,2,256,128]{3,2,1,0:T(8,128)S(1)}, f32[3,8,128]{2,1,0:T(8,128)S(1)}) custom-call(f32[3,128,1024]{2,1,0:T(8,128)} %src_hbm.1, s32[128,1024]{1,0:T(8,128)} %lab_hbm.1), custom_call_target="tpu_custom_call" | custom-call | tf_op jit(solution)/shard_map/pallas_call | solution.py:762
  14.8 1.0 %shard_map.58 = (f32[128,1024]{1,0:T(8,128)}, f32[64,512]{1,0:T(8,128)}, f32[256,256]{1,0:T(8,128)}, f32[128,128]{1,0:T(8,128)}) custom-call(f32[3,9,144,128]{3,2,1,0:T(8,128)S(1)} %get-tuple-element.8.vec, f32[3,4,64,128]{3,2,1,0:T(8,128)S(1)} %get-tuple-element.9.fines, f32[3,2,256,128]{3,2,1,0:T(8,128)S(1)} %get-tuple-element.10.mids, ...), custom_call_target="tpu_custom_call" | custom-call | tf_op jit(solution)/shard_map/pallas_call | solution.py:810

commit v4 on v3

--- a/solution.py
+++ b/solution.py
@@ -8,7 +8,6 @@
 from jax.sharding import PartitionSpec as P
 
 ITERS = 3
-DIRECT = 3
 MESH = pl.DeviceIdType.MESH
 HALO = 4
 TOP = 8
@@ -159,8 +158,8 @@
     n_row, n_col, rows, cols, kinds,
     src_hbm, lab_hbm, vec, fines, mids, coord_ref,
     src, lab, edge, edge_lab, pack_up, pack_down, pack_c, pack_d, got_up, got_down, got_c, got_d,
-    part, moment, band, patch, sides, load_sem, send_sem, recv_sem, chain, mom_send, mom_recv, mid_send, near_recv, far_recv,
-    fwd_send, fwd_recv, patch_send, patch_recv,
+    part, moment, band, patch, sides, token, load_sem, send_sem, recv_sem, chain,
+    tell_send, mom_recv, mid_send, near_recv, far_recv, fwd_recv, patch_recv,
 ):
     tiles = cols // LANES
     side_tile = tiles
@@ -206,15 +205,15 @@
         lanes = pl.ds(t * LANES, LANES)
         if k < kinds:
             return pltpu.make_async_copy(
-                src_hbm.at[k, :, lanes], src.at[k, t, body_rows], load_sem.at[2 * wave])
+                src_hbm.at[k, :, lanes], src.at[k, t, body_rows], load_sem.at[wave])
         return pltpu.make_async_copy(
-            lab_hbm.at[:, lanes], lab.at[t, body_rows], load_sem.at[2 * wave + 1])
+            lab_hbm.at[:, lanes], lab.at[t, body_rows], load_sem.at[wave])
 
     def edge_load(k, side):
         here = pl.ds(0 if side == 0 else rows - 8, 8)
         if k < kinds:
-            return pltpu.make_async_copy(src_hbm.at[k, here], edge.at[k, side], load_sem.at[4])
-        return pltpu.make_async_copy(lab_hbm.at[here], edge_lab.at[side], load_sem.at[5])
+            return pltpu.make_async_copy(src_hbm.at[k, here], edge.at[k, side], load_sem.at[0])
+        return pltpu.make_async_copy(lab_hbm.at[here], edge_lab.at[side], load_sem.at[0])
 
     def wait_bytes(ref, sem):
         pltpu.make_async_copy(ref, ref, sem).wait()
@@ -245,10 +244,7 @@
 
     n_pack = HALO * (kinds + 1)
     with jax.named_scope("wait_first"):
-        wait_bytes(edge, load_sem.at[4])
-        wait_bytes(edge_lab, load_sem.at[5])
-        wait_bytes(src.at[:, pl.ds(0, 2), body_rows], load_sem.at[0])
-        wait_bytes(lab.at[pl.ds(0, 2), body_rows], load_sem.at[1])
+        wait_bytes(token.at[pl.ds(0, 2 * (kinds + 1) * (8 * tiles + rows))], load_sem.at[0])
     with jax.named_scope("pack"):
         for side in range(2):
             for k in range(kinds + 1):
@@ -284,32 +280,38 @@
     with jax.named_scope("barrier"):
         pl.semaphore_wait(barrier, greeters)
 
-    sends = []
-    for i, (dr, dc) in enumerate(SIDES):
+    def place(dr, dc):
+        return (0 if dr < 0 else 1) if dc == 0 else 2 if dr == 0 else 3
+
+    for dr, dc in SIDES:
         mine_r, mine_c = (0 if dr < 0 else 1), (0 if dc < 0 else 1)
         if dc == 0:
-            source, target, here = (
-                (pack_up, got_up, got_down) if dr < 0 else (pack_down, got_down, got_up))
+            source, target = (pack_up, got_up) if dr < 0 else (pack_down, got_down)
         elif dr == 0:
-            source, target, here = pack_c.at[mine_c], got_c.at[1 - mine_c], got_c.at[mine_c]
+            source, target = pack_c.at[mine_c], got_c.at[1 - mine_c]
         else:
             source = pack_d.at[mine_r, mine_c]
-            target, here = got_d.at[1 - mine_r, 1 - mine_c], got_d.at[mine_r, mine_c]
-        opposite = SIDES.index((-dr, -dc))
+            target = got_d.at[1 - mine_r, 1 - mine_c]
         device = (
             jnp.clip(row + dr, 0, n_row - 1),
             jnp.clip(col + dc, 0, n_col - 1),
         )
-        copy = pltpu.make_async_remote_copy(
-            src_ref=source, dst_ref=target, send_sem=send_sem.at[i],
-            recv_sem=recv_sem.at[opposite], device_id=device, device_id_type=MESH,
-        )
-        back = pltpu.make_async_remote_copy(
-            src_ref=source, dst_ref=here, send_sem=send_sem.at[i],
-            recv_sem=recv_sem.at[i], device_id=device, device_id_type=MESH,
-        )
-        sends.append((there[dr, dc], copy, back))
-        pl.when(there[dr, dc])(copy.start)
+        pl.when(there[dr, dc])(pltpu.make_async_remote_copy(
+            src_ref=source, dst_ref=target, send_sem=send_sem.at[place(dr, dc)],
+            recv_sem=recv_sem.at[place(-dr, -dc)], device_id=device, device_id_type=MESH,
+        ).start)
+
+    def wait_halos(sem, above, below):
+        pl.when(there[-1, 0])(lambda: wait_bytes(above, sem.at[0]))
+        pl.when(there[1, 0])(lambda: wait_bytes(below, sem.at[1]))
+        beside_rows = jnp.where(there[-1, 0], 1, 0) + jnp.where(there[1, 0], 1, 0)
+        beside_cols = jnp.where(there[0, -1], 1, 0) + jnp.where(there[0, 1], 1, 0)
+        corners = beside_rows * beside_cols
+        pl.when(beside_cols == 2)(lambda: wait_bytes(got_c, sem.at[2]))
+        pl.when(beside_cols == 1)(lambda: wait_bytes(got_c.at[0], sem.at[2]))
+        pl.when(corners == 4)(lambda: wait_bytes(got_d, sem.at[3]))
+        pl.when(corners == 2)(lambda: wait_bytes(got_d.at[0], sem.at[3]))
+        pl.when(corners == 1)(lambda: wait_bytes(got_d.at[0, 0], sem.at[3]))
 
     def pass_on(dc):
         pl.semaphore_signal(
@@ -329,8 +331,7 @@
     pl.when(jnp.logical_and(last_col, there[0, -1]))(lambda: pass_on(-1))
 
     with jax.named_scope("wait_later"):
-        wait_bytes(src.at[:, pl.ds(1, tiles - 2), body_rows], load_sem.at[2])
-        wait_bytes(lab.at[pl.ds(1, tiles - 2), body_rows], load_sem.at[3])
+        wait_bytes(token.at[pl.ds(0, (kinds + 1) * (tiles - 2) * rows)], load_sem.at[1])
     groups = rows // 8
     lane_r = lane_of((tiles, 8, LANES))
     lane_t = lane_of((8, LANES))
@@ -374,8 +375,8 @@
     quad = rows // 4
     pool4, pool2 = pool_matrix(4), pool_matrix(2)
 
-    def some(w, count):
-        return mids.at[w, :, pl.ds(0, count * quad)]
+    def blocks(count):
+        return mids.at[:, :, pl.ds(0, count * quad)]
 
     def hand(w, owner, target, send, recv):
         block = mids.at[w, :, pl.ds(pl.multiple_of(owner * quad, 8), quad)]
@@ -387,19 +388,13 @@
         return 2 * q + core
 
     def to_partner(w, owner):
-        hand(w, owner, partner, fwd_send, fwd_recv)
-
+        hand(w, owner, partner, mid_send, fwd_recv)
+
+    others = [lax.rem(chip + step, chips) for step in range(1, chips)]
     if chips == 4:
-        beside = [chip + 1 - 2 * lax.rem(chip, 2), chip + 2 - 4 * lax.div(chip, 2)]
-        across = 3 - chip
-        via = same_core(jnp.where(core == 0, beside[0], beside[1]))
-        onward = same_core(jnp.where(core == 0, beside[1], beside[0]))
-        near = [same_core(q) for q in beside]
-    else:
-        near = []
-        for step in range(1, chips):
-            q = chip + step
-            near.append(same_core(jnp.where(q >= chips, q - chips, q)))
+        others = [chip + 1 - 2 * lax.rem(chip, 2), chip + 2 - 4 * lax.div(chip, 2), 3 - chip]
+    others = [same_core(q) for q in others]
+    near, far = others[:-1], others[-1]
 
     def send_early(w):
         own = pooled(
@@ -411,9 +406,8 @@
             mids[w, q, pl.ds(pl.multiple_of(row * quad, 8), quad), :] = own[
                 q * quad:(q + 1) * quad]
         for target in near:
-            hand(w, row, target, mid_send, near_recv.at[w])
-        if chips == 4 and w < DIRECT:
-            hand(w, row, same_core(across), mid_send, far_recv.at[w])
+            hand(w, row, target, mid_send, near_recv)
+        hand(w, row, far, mid_send, far_recv)
         to_partner(w, row)
 
     with jax.named_scope("main_v"):
@@ -477,8 +471,7 @@
         pl.when(jnp.logical_and(inner_col, upper_half))(lambda: relay(-1))
 
     with jax.named_scope("wait_halo"):
-        for exists, copy, back in sends:
-            pl.when(exists)(back.wait_recv)
+        wait_halos(recv_sem, got_down, got_up)
 
     with jax.named_scope("unpack"):
         for k in range(kinds + 1):
@@ -564,7 +557,7 @@
 
         def tell(r, c):
             pltpu.make_async_remote_copy(
-                src_ref=moment.at[me], dst_ref=moment.at[me], send_sem=mom_send, recv_sem=mom_recv,
+                src_ref=moment.at[me], dst_ref=moment.at[me], send_sem=tell_send, recv_sem=mom_recv,
                 device_id=(r, c), device_id_type=MESH).start()
 
         def tell_block(c):
@@ -609,16 +602,15 @@
             at = len(lines_of) + w
             patch[row, at:at + 1, :] = jnp.where(row_lane < 2 * quad, left, right) * (1.0 / 16)
         for_other_rows(lambda r: pltpu.make_async_remote_copy(
-            src_ref=patch.at[row], dst_ref=patch.at[row], send_sem=patch_send,
+            src_ref=patch.at[row], dst_ref=patch.at[row], send_sem=tell_send,
             recv_sem=patch_recv, device_id=(r, col), device_id_type=MESH).start())
 
     with jax.named_scope("near"):
+        wait_bytes(blocks(len(near)), near_recv)
         for w in range(ITERS):
-            wait_bytes(some(w, len(near)), near_recv.at[w])
-            if chips == 4 and w >= DIRECT:
-                hand(w, via, onward, mid_send, far_recv.at[w])
             for owner in near:
                 to_partner(w, owner)
+
     with jax.named_scope("merge"):
         for w in range(ITERS):
             side = vec[w, side_tile, body_rows]
@@ -641,11 +633,10 @@
     with jax.named_scope("tell_first"):
         pl.when(jnp.logical_and(first_col, there[0, 1]))(tell_rest)
 
-    if chips == 4:
-        with jax.named_scope("far"):
-            for w in range(ITERS):
-                wait_bytes(some(w, 1), far_recv.at[w])
-                to_partner(w, same_core(across))
+    with jax.named_scope("far"):
+        wait_bytes(blocks(1), far_recv)
+        for w in range(ITERS):
+            to_partner(w, far)
 
     with jax.named_scope("wait_patch"):
         patches = patch.at[pl.ds(0, n_row - 1)]
@@ -661,11 +652,9 @@
                     sides[w, end, pl.ds(2 * pair * quad, 2 * quad), :] = jnp.broadcast_to(
                         part_here, (2 * quad, LANES))
 
-    every_core = mids.at[:, :, pl.ds(0, chips * quad)]
     with jax.named_scope("wait_forwards"):
-        wait_bytes(mids.at[:, :, pl.ds(0, (chips - 1) * quad)], mid_send)
-        wait_bytes(every_core, fwd_send)
-        wait_bytes(every_core, fwd_recv)
+        wait_bytes(blocks(2 * chips - 1), mid_send)
+        wait_bytes(blocks(chips), fwd_recv)
     with jax.named_scope("apply"):
         for owner in range(n_row):
             for at, (w, e, q) in enumerate(lines_of):
@@ -690,10 +679,8 @@
             coord_ref[w] = jnp.broadcast_to(0.25 ** w * c, (8, LANES))
 
     with jax.named_scope("wait_sends"):
-        for exists, copy, back in sends:
-            pl.when(exists)(copy.wait_send)
-        wait_bytes(everyone, mom_send)
-        wait_bytes(patches, patch_send)
+        wait_halos(send_sem, got_up, got_down)
+        wait_bytes(token.at[pl.ds(0, n - 1 + (n_row - 1) * patch.shape[1])], tell_send)
 
 
 def finish_kernel(
@@ -756,6 +743,7 @@
     vmem = pl.BlockSpec(memory_space=pltpu.VMEM)
     hbm = pl.BlockSpec(memory_space=pltpu.HBM)
     up_lines, down_lines = ((kinds * d + d - 1) * tiles for d in (HALO, HALO - 1))
+    token_lines = (kinds + 1) * max(2 * (8 * tiles + rows), (tiles - 2) * rows)
     mid_rows, coarse_rows = n_row * rows // 4, n_row * rows // 8
     chips = n_row // 2
     dma = pltpu.SemaphoreType.DMA
@@ -787,15 +775,14 @@
             pltpu.VMEM((4, ITERS * (tiles // 2), LANES), f32),
             pltpu.VMEM((n_row, ITERS * (tiles // 2) + 4, LANES), f32),
             pltpu.VMEM((ITERS, 2, mid_rows, LANES), f32),
-            dma((6,)),
-            dma((8,)),
-            dma((8,)),
+            pltpu.VMEM((token_lines, LANES), f32),
+            dma((2,)),
+            dma((4,)),
+            dma((4,)),
             pltpu.SemaphoreType.REGULAR((2,)),
             dma,
             dma,
             dma,
-            dma((ITERS,)),
-            dma((ITERS,)),
             dma,
             dma,
             dma,

time: 16 us -> 15.8 us (0.988)
  Pallas kernels: 15.2 us -> 15 us
    pallas_call x1, Pallas kernels: 14.2 us -> 14 us  [per_device(): pl.pallas_call(functools.partial(gather_kernel, n_row, n_col, rows, cols,...]
where the time goes in v4:
time: 15.8 us; the launch traced here: 15.7 us
  Pallas kernels  15 us (95%)
  between operations  0.64 us (4%)
    pallas_call x1, Pallas kernels, per_device(): pl.pallas_call(functools.partial(gather_kernel, n_row, n_col, rows, cols,...  14 us
    pallas_call x1, Pallas kernels, per_device(): pl.pallas_call(functools.partial(finish_kernel, rows, cols), out_shape=(j...  1.02 us

profile of v4, /device:TPU:0, one launch (start us, length us, event | category | flops | bytes accessed | tf_op | source)
XLA Modules:
  0.0 15.7 jit_solution(3719024934692547467)
XLA Ops:
  0.6 14.0 %shard_map.57 = (f32[3,9,144,128]{3,2,1,0:T(8,128)S(1)}, f32[3,4,64,128]{3,2,1,0:T(8,128)S(1)}, f32[3,2,256,128]{3,2,1,0:T(8,128)S(1)}, f32[3,8,128]{2,1,0:T(8,128)S(1)}) custom-call(f32[3,128,1024]{2,1,0:T(8,128)} %src_hbm.1, s32[128,1024]{1,0:T(8,128)} %lab_hbm.1), custom_call_target="tpu_custom_call" | custom-call | tf_op jit(solution)/shard_map/pallas_call | solution.py:750
  14.6 1.0 %shard_map.58 = (f32[128,1024]{1,0:T(8,128)}, f32[64,512]{1,0:T(8,128)}, f32[256,256]{1,0:T(8,128)}, f32[128,128]{1,0:T(8,128)}) custom-call(f32[3,9,144,128]{3,2,1,0:T(8,128)S(1)} %get-tuple-element.8.vec, f32[3,4,64,128]{3,2,1,0:T(8,128)S(1)} %get-tuple-element.9.fines, f32[3,2,256,128]{3,2,1,0:T(8,128)S(1)} %get-tuple-element.10.mids, ...), custom_call_target="tpu_custom_call" | custom-call | tf_op jit(solution)/shard_map/pallas_call | solution.py:797

commit v5 on v4

--- a/solution.py
+++ b/solution.py
@@ -159,7 +159,7 @@
     src_hbm, lab_hbm, vec, fines, mids, coord_ref,
     src, lab, edge, edge_lab, pack_up, pack_down, pack_c, pack_d, got_up, got_down, got_c, got_d,
     part, moment, band, patch, sides, token, load_sem, send_sem, recv_sem, chain,
-    tell_send, mom_recv, mid_send, near_recv, far_recv, fwd_recv, patch_recv,
+    tell_send, mom_recv, mid_send, chip_recv, fwd_recv, patch_recv,
 ):
     tiles = cols // LANES
     side_tile = tiles
@@ -301,17 +301,20 @@
             recv_sem=recv_sem.at[place(-dr, -dc)], device_id=device, device_id_type=MESH,
         ).start)
 
-    def wait_halos(sem, above, below):
+    beside_rows = jnp.where(there[-1, 0], 1, 0) + jnp.where(there[1, 0], 1, 0)
+    beside_cols = jnp.where(there[0, -1], 1, 0) + jnp.where(there[0, 1], 1, 0)
+    corners = beside_rows * beside_cols
+
+    def wait_rows(sem, above, below):
         pl.when(there[-1, 0])(lambda: wait_bytes(above, sem.at[0]))
         pl.when(there[1, 0])(lambda: wait_bytes(below, sem.at[1]))
-        beside_rows = jnp.where(there[-1, 0], 1, 0) + jnp.where(there[1, 0], 1, 0)
-        beside_cols = jnp.where(there[0, -1], 1, 0) + jnp.where(there[0, 1], 1, 0)
-        corners = beside_rows * beside_cols
-        pl.when(beside_cols == 2)(lambda: wait_bytes(got_c, sem.at[2]))
-        pl.when(beside_cols == 1)(lambda: wait_bytes(got_c.at[0], sem.at[2]))
         pl.when(corners == 4)(lambda: wait_bytes(got_d, sem.at[3]))
         pl.when(corners == 2)(lambda: wait_bytes(got_d.at[0], sem.at[3]))
         pl.when(corners == 1)(lambda: wait_bytes(got_d.at[0, 0], sem.at[3]))
+
+    def wait_columns(sem):
+        pl.when(beside_cols == 2)(lambda: wait_bytes(got_c, sem.at[2]))
+        pl.when(beside_cols == 1)(lambda: wait_bytes(got_c.at[0], sem.at[2]))
 
     def pass_on(dc):
         pl.semaphore_signal(
@@ -375,8 +378,8 @@
     quad = rows // 4
     pool4, pool2 = pool_matrix(4), pool_matrix(2)
 
-    def blocks(count):
-        return mids.at[:, :, pl.ds(0, count * quad)]
+    def blocks(count, w=slice(None)):
+        return mids.at[w, :, pl.ds(0, count * quad)]
 
     def hand(w, owner, target, send, recv):
         block = mids.at[w, :, pl.ds(pl.multiple_of(owner * quad, 8), quad)]
@@ -392,9 +395,8 @@
 
     others = [lax.rem(chip + step, chips) for step in range(1, chips)]
     if chips == 4:
-        others = [chip + 1 - 2 * lax.rem(chip, 2), chip + 2 - 4 * lax.div(chip, 2), 3 - chip]
+        others = [3 - chip, chip + 1 - 2 * lax.rem(chip, 2), chip + 2 - 4 * lax.div(chip, 2)]
     others = [same_core(q) for q in others]
-    near, far = others[:-1], others[-1]
 
     def send_early(w):
         own = pooled(
@@ -405,9 +407,8 @@
         for q in range(tiles // 4):
             mids[w, q, pl.ds(pl.multiple_of(row * quad, 8), quad), :] = own[
                 q * quad:(q + 1) * quad]
-        for target in near:
-            hand(w, row, target, mid_send, near_recv)
-        hand(w, row, far, mid_send, far_recv)
+        for target in others:
+            hand(w, row, target, mid_send, chip_recv.at[w])
         to_partner(w, row)
 
     with jax.named_scope("main_v"):
@@ -470,10 +471,10 @@
         pl.when(inner_col)(lambda: relay(1))
         pl.when(jnp.logical_and(inner_col, upper_half))(lambda: relay(-1))
 
-    with jax.named_scope("wait_halo"):
-        wait_halos(recv_sem, got_down, got_up)
-
-    with jax.named_scope("unpack"):
+    with jax.named_scope("wait_cols"):
+        wait_columns(recv_sem)
+
+    with jax.named_scope("unpack_cols"):
         for k in range(kinds + 1):
             at = pl.ds(HALO * k, HALO)
             right = jnp.where(last_col, 0.0, got_c[1, at, :])
@@ -484,6 +485,55 @@
             else:
                 lab[side_tile, body_rows, 0:2 * HALO] = turned.astype(jnp.int32)
         corner_lane = lane_of((HALO, LANES))
+
+    off_lane = ((lane_t < HALO) & last_col) | ((lane_t >= HALO) & (lane_t < 2 * HALO) & first_col)
+    off_top = (line_t < HALO) & first_row
+    off_bottom = (line_t >= HALO) & last_row
+    ends = ((TOP - HALO, off_top), (TOP + rows - HALO, off_bottom))
+
+    def stage(which, tile, start, beside):
+        if which == 0:
+            return right_side(src, lab, tile, start, beside)
+        return applied(which - 1, tile, start, beside)
+
+    def side_groups(which, begin, end):
+        for i in range(begin, end):
+            start = TOP - HALO + 8 * i
+            off = off_lane
+            if i == 0:
+                off = off | off_top
+            if i == groups:
+                off = off | off_bottom
+            save(which, side_tile, start, jnp.where(
+                off, 0.0, stage(which, side_tile, start, beside_tile)))
+
+    def side_inner(which):
+        begin = TOP + HALO + 8 * which
+        count = groups - 1 - 2 * which
+        whole_loop(count, lambda i: save(
+            which, side_tile, begin + 8 * i, jnp.where(
+                off_lane, 0.0, stage(which, side_tile, begin + 8 * i, beside_tile))))
+
+    on_side = ((lane_t >= 2 * HALO) & (lane_t < 3 * HALO)) | (lane_t >= LANES - HALO)
+
+    def side_sums(begin, end, sums):
+        def body(i, sums):
+            new = products(
+                side_tile, TOP + 8 * (begin + i), right_tile, lambda p: jnp.where(on_side, p, 0.0))
+            return tuple(s + p for s, p in zip(sums, new))
+
+        return list(lax.fori_loop(0, end - begin, body, tuple(sums), unroll=end - begin))
+
+    with jax.named_scope("side_inner"):
+        for which in range(ITERS):
+            side_inner(which)
+        for i, s in enumerate(side_sums(ITERS, groups - ITERS, [part[i] for i in range(2 * ITERS)])):
+            part[i] = s
+
+    with jax.named_scope("wait_halo"):
+        wait_rows(recv_sem, got_down, got_up)
+
+    with jax.named_scope("unpack"):
         for side in range(2):
             missing = first_row if side == 0 else last_row
             got = got_down if side == 0 else got_up
@@ -509,40 +559,17 @@
                     else:
                         lab[t, pl.ds(base, depth), :] = value.astype(jnp.int32)
 
-    off_lane = ((lane_t < HALO) & last_col) | ((lane_t >= HALO) & (lane_t < 2 * HALO) & first_col)
-    off_top = (line_t < HALO) & first_row
-    off_bottom = (line_t >= HALO) & last_row
-    ends = ((TOP - HALO, off_top), (TOP + rows - HALO, off_bottom))
-
-    def frame(which):
-        def value(tile, start, beside):
-            if which == 0:
-                return right_side(src, lab, tile, start, beside)
-            return applied(which - 1, tile, start, beside)
-
-        def side_group(start, off):
-            save(which, side_tile, start, jnp.where(off, 0.0, value(side_tile, start, beside_tile)))
-
-        side_group(ends[0][0], off_top | off_lane)
-        whole_loop(groups - 1, lambda i: side_group(TOP + HALO + 8 * i, off_lane))
-        side_group(ends[1][0], off_bottom | off_lane)
-        for start, off in ends:
-            save(which, main, start, jnp.where(off[None], 0.0, value(main, start, beside_ring)))
-
     with jax.named_scope("frames"):
         for which in range(ITERS):
-            frame(which)
+            side_groups(which, 0, 1 + which)
+            side_groups(which, groups - which, groups + 1)
+            for start, off in ends:
+                save(which, main, start, jnp.where(
+                    off[None], 0.0, stage(which, main, start, beside_ring)))
 
     with jax.named_scope("moments"):
-        sums = [part[i] for i in range(2 * ITERS)]
-        on_side = ((lane_t >= 2 * HALO) & (lane_t < 3 * HALO)) | (lane_t >= LANES - HALO)
-
-        def side_body(i, sums):
-            new = products(
-                side_tile, TOP + 8 * i, right_tile, lambda p: jnp.where(on_side, p, 0.0))
-            return tuple(s + p for s, p in zip(sums, new))
-
-        sums = lax.fori_loop(0, groups, side_body, tuple(sums), unroll=groups)
+        sums = side_sums(0, ITERS, [part[i] for i in range(2 * ITERS)])
+        sums = side_sums(groups - ITERS, groups, sums)
         for (start, _), on in zip(ends, (line_t >= HALO, line_t < HALO)):
             new = products(main, start, right_ring, lambda p: jnp.where(on[None], keep_main(p), 0.0))
             sums = [s + fold(p) for s, p in zip(sums, new)]
@@ -605,12 +632,6 @@
             src_ref=patch.at[row], dst_ref=patch.at[row], send_sem=tell_send,
             recv_sem=patch_recv, device_id=(r, col), device_id_type=MESH).start())
 
-    with jax.named_scope("near"):
-        wait_bytes(blocks(len(near)), near_recv)
-        for w in range(ITERS):
-            for owner in near:
-                to_partner(w, owner)
-
     with jax.named_scope("merge"):
         for w in range(ITERS):
             side = vec[w, side_tile, body_rows]
@@ -633,10 +654,11 @@
     with jax.named_scope("tell_first"):
         pl.when(jnp.logical_and(first_col, there[0, 1]))(tell_rest)
 
-    with jax.named_scope("far"):
-        wait_bytes(blocks(1), far_recv)
+    with jax.named_scope("near"):
         for w in range(ITERS):
-            to_partner(w, far)
+            wait_bytes(blocks(chips - 1, w), chip_recv.at[w])
+            for owner in others:
+                to_partner(w, owner)
 
     with jax.named_scope("wait_patch"):
         patches = patch.at[pl.ds(0, n_row - 1)]
@@ -679,7 +701,8 @@
             coord_ref[w] = jnp.broadcast_to(0.25 ** w * c, (8, LANES))
 
     with jax.named_scope("wait_sends"):
-        wait_halos(send_sem, got_up, got_down)
+        wait_rows(send_sem, got_up, got_down)
+        wait_columns(send_sem)
         wait_bytes(token.at[pl.ds(0, n - 1 + (n_row - 1) * patch.shape[1])], tell_send)
 
 
@@ -783,8 +806,7 @@
             dma,
             dma,
             dma,
-            dma,
-            dma,
+            dma((ITERS,)),
             dma,
             dma,
         ],

time: 15.8 us -> 15.7 us (level)
  no operation moved by 1% of the time
where the time goes in v5:
time: 15.7 us; the launch traced here: 15.6 us
  Pallas kernels  14.9 us (95%)
  between operations  0.64 us (4%)
    pallas_call x1, Pallas kernels, per_device(): pl.pallas_call(functools.partial(gather_kernel, n_row, n_col, rows, cols,...  13.9 us
    pallas_call x1, Pallas kernels, per_device(): pl.pallas_call(functools.partial(finish_kernel, rows, cols), out_shape=(j...  1.02 us

profile of v5, /device:TPU:0, one launch (start us, length us, event | category | flops | bytes accessed | tf_op | source)
XLA Modules:
  0.0 15.6 jit_solution(855498177124257625)
XLA Ops:
  0.6 13.9 %shard_map.57 = (f32[3,9,144,128]{3,2,1,0:T(8,128)S(1)}, f32[3,4,64,128]{3,2,1,0:T(8,128)S(1)}, f32[3,2,256,128]{3,2,1,0:T(8,128)S(1)}, f32[3,8,128]{2,1,0:T(8,128)S(1)}) custom-call(f32[3,128,1024]{2,1,0:T(8,128)} %src_hbm.1, s32[128,1024]{1,0:T(8,128)} %lab_hbm.1), custom_call_target="tpu_custom_call" | custom-call | tf_op jit(solution)/shard_map/pallas_call | solution.py:773
  14.5 1.0 %shard_map.58 = (f32[128,1024]{1,0:T(8,128)}, f32[64,512]{1,0:T(8,128)}, f32[256,256]{1,0:T(8,128)}, f32[128,128]{1,0:T(8,128)}) custom-call(f32[3,9,144,128]{3,2,1,0:T(8,128)S(1)} %get-tuple-element.8.vec, f32[3,4,64,128]{3,2,1,0:T(8,128)S(1)} %get-tuple-element.9.fines, f32[3,2,256,128]{3,2,1,0:T(8,128)S(1)} %get-tuple-element.10.mids, ...), custom_call_target="tpu_custom_call" | custom-call | tf_op jit(solution)/shard_map/pallas_call | solution.py:819

commit v6 on v5

--- a/solution.py
+++ b/solution.py
@@ -12,7 +12,7 @@
 HALO = 4
 TOP = 8
 LANES = 128
-SIDES = ((-1, -1), (-1, 1), (1, -1), (1, 1), (-1, 0), (1, 0), (0, -1), (0, 1))
+SIDES = ((1, 1), (1, -1), (-1, 1), (-1, -1), (1, 0), (-1, 0), (0, 1), (0, -1))
 
 
 def lane_of(shape):
@@ -196,7 +196,7 @@
         pl.semaphore_signal(barrier, inc=1, device_id=(r, c), device_id_type=MESH)
 
     greeters = n_row - 1
-    for dr, dc in SIDES:
+    for dr, dc in ((-r, -c) for r, c in SIDES):
         if dc:
             pl.when(there[dr, dc])(functools.partial(
                 greet, jnp.clip(row + dr, 0, n_row - 1), jnp.clip(col + dc, 0, n_col - 1)))
@@ -366,6 +366,8 @@
             src, lab, main, TOP + 8 * i,
             lines(vec, (1, main), TOP + 8 * i), lines(vec, (2, main), TOP + 8 * i))))
 
+    pl.when(jnp.logical_and(inner_col, jnp.logical_not(upper_half)))(lambda: relay(1))
+
     def inner(which):
         whole_loop(groups, lambda i: save(
             which, main, TOP + 8 * i, applied(which - 1, main, TOP + 8 * i, beside_ring)))
@@ -468,7 +470,7 @@
                     wide_lane < LANES // 2, pltpu.roll(first, 2 * HALO, axis=1), last)
 
     with jax.named_scope("relay"):
-        pl.when(inner_col)(lambda: relay(1))
+        pl.when(jnp.logical_and(inner_col, upper_half))(lambda: relay(1))
         pl.when(jnp.logical_and(inner_col, upper_half))(lambda: relay(-1))
 
     with jax.named_scope("wait_cols"):

time: 15.7 us -> 15.7 us (level)
  no operation moved by 1% of the time
where the time goes in v6:
time: 15.7 us; the launch traced here: 15.6 us
  Pallas kernels  14.9 us (95%)
  between operations  0.64 us (4%)
    pallas_call x1, Pallas kernels, per_device(): pl.pallas_call(functools.partial(gather_kernel, n_row, n_col, rows, cols,...  13.9 us
    pallas_call x1, Pallas kernels, per_device(): pl.pallas_call(functools.partial(finish_kernel, rows, cols), out_shape=(j...  1.02 us

profile of v6, /device:TPU:0, one launch (start us, length us, event | category | flops | bytes accessed | tf_op | source)
XLA Modules:
  0.0 15.6 jit_solution(2637331299340647079)
XLA Ops:
  0.6 13.9 %shard_map.57 = (f32[3,9,144,128]{3,2,1,0:T(8,128)S(1)}, f32[3,4,64,128]{3,2,1,0:T(8,128)S(1)}, f32[3,2,256,128]{3,2,1,0:T(8,128)S(1)}, f32[3,8,128]{2,1,0:T(8,128)S(1)}) custom-call(f32[3,128,1024]{2,1,0:T(8,128)} %src_hbm.1, s32[128,1024]{1,0:T(8,128)} %lab_hbm.1), custom_call_target="tpu_custom_call" | custom-call | tf_op jit(solution)/shard_map/pallas_call | solution.py:775
  14.5 1.0 %shard_map.58 = (f32[128,1024]{1,0:T(8,128)}, f32[64,512]{1,0:T(8,128)}, f32[256,256]{1,0:T(8,128)}, f32[128,128]{1,0:T(8,128)}) custom-call(f32[3,9,144,128]{3,2,1,0:T(8,128)S(1)} %get-tuple-element.8.vec, f32[3,4,64,128]{3,2,1,0:T(8,128)S(1)} %get-tuple-element.9.fines, f32[3,2,256,128]{3,2,1,0:T(8,128)S(1)} %get-tuple-element.10.mids, ...), custom_call_target="tpu_custom_call" | custom-call | tf_op jit(solution)/shard_map/pallas_call | solution.py:821

commit v7 on v6

--- a/solution.py
+++ b/solution.py
@@ -159,8 +159,9 @@
     src_hbm, lab_hbm, vec, fines, mids, coord_ref,
     src, lab, edge, edge_lab, pack_up, pack_down, pack_c, pack_d, got_up, got_down, got_c, got_d,
     part, moment, band, patch, sides, token, load_sem, send_sem, recv_sem, chain,
-    tell_send, mom_recv, mid_send, chip_recv, fwd_recv, patch_recv,
+    mom_recv, chip_recv, fwd_recv, patch_recv,
 ):
+    tell_send, mid_send = load_sem.at[0], load_sem.at[1]
     tiles = cols // LANES
     side_tile = tiles
     main = slice(0, tiles)
@@ -380,8 +381,8 @@
     quad = rows // 4
     pool4, pool2 = pool_matrix(4), pool_matrix(2)
 
-    def blocks(count, w=slice(None)):
-        return mids.at[w, :, pl.ds(0, count * quad)]
+    def blocks(count):
+        return mids.at[:, :, pl.ds(0, count * quad)]
 
     def hand(w, owner, target, send, recv):
         block = mids.at[w, :, pl.ds(pl.multiple_of(owner * quad, 8), quad)]
@@ -410,7 +411,7 @@
             mids[w, q, pl.ds(pl.multiple_of(row * quad, 8), quad), :] = own[
                 q * quad:(q + 1) * quad]
         for target in others:
-            hand(w, row, target, mid_send, chip_recv.at[w])
+            hand(w, row, target, mid_send, chip_recv)
         to_partner(w, row)
 
     with jax.named_scope("main_v"):
@@ -657,8 +658,8 @@
         pl.when(jnp.logical_and(first_col, there[0, 1]))(tell_rest)
 
     with jax.named_scope("near"):
+        wait_bytes(blocks(chips - 1), chip_recv)
         for w in range(ITERS):
-            wait_bytes(blocks(chips - 1, w), chip_recv.at[w])
             for owner in others:
                 to_partner(w, owner)
 
@@ -808,8 +809,6 @@
             dma,
             dma,
             dma,
-            dma((ITERS,)),
-            dma,
             dma,
         ],
         compiler_params=pltpu.CompilerParams(

time: 15.7 us -> 15.7 us (level)
  no operation moved by 1% of the time
where the time goes in v7:
time: 15.7 us; the launch traced here: 15.5 us
  Pallas kernels  14.9 us (95%)
  between operations  0.64 us (4%)
    pallas_call x1, Pallas kernels, per_device(): pl.pallas_call(functools.partial(gather_kernel, n_row, n_col, rows, cols,...  13.9 us
    pallas_call x1, Pallas kernels, per_device(): pl.pallas_call(functools.partial(finish_kernel, rows, cols), out_shape=(j...  1.02 us

profile of v7, /device:TPU:0, one launch (start us, length us, event | category | flops | bytes accessed | tf_op | source)
XLA Modules:
  0.0 15.5 jit_solution(1912205527149743375)
XLA Ops:
  0.6 13.9 %shard_map.57 = (f32[3,9,144,128]{3,2,1,0:T(8,128)S(1)}, f32[3,4,64,128]{3,2,1,0:T(8,128)S(1)}, f32[3,2,256,128]{3,2,1,0:T(8,128)S(1)}, f32[3,8,128]{2,1,0:T(8,128)S(1)}) custom-call(f32[3,128,1024]{2,1,0:T(8,128)} %src_hbm.1, s32[128,1024]{1,0:T(8,128)} %lab_hbm.1), custom_call_target="tpu_custom_call" | custom-call | tf_op jit(solution)/shard_map/pallas_call | solution.py:776
  14.5 1.0 %shard_map.58 = (f32[128,1024]{1,0:T(8,128)}, f32[64,512]{1,0:T(8,128)}, f32[256,256]{1,0:T(8,128)}, f32[128,128]{1,0:T(8,128)}) custom-call(f32[3,9,144,128]{3,2,1,0:T(8,128)S(1)} %get-tuple-element.8.vec, f32[3,4,64,128]{3,2,1,0:T(8,128)S(1)} %get-tuple-element.9.fines, f32[3,2,256,128]{3,2,1,0:T(8,128)S(1)} %get-tuple-element.10.mids, ...), custom_call_target="tpu_custom_call" | custom-call | tf_op jit(solution)/shard_map/pallas_call | solution.py:820

commit v8 on v7

--- a/solution.py
+++ b/solution.py
@@ -528,10 +528,8 @@
         return list(lax.fori_loop(0, end - begin, body, tuple(sums), unroll=end - begin))
 
     with jax.named_scope("side_inner"):
-        for which in range(ITERS):
+        for which in range(ITERS - 1):
             side_inner(which)
-        for i, s in enumerate(side_sums(ITERS, groups - ITERS, [part[i] for i in range(2 * ITERS)])):
-            part[i] = s
 
     with jax.named_scope("wait_halo"):
         wait_rows(recv_sem, got_down, got_up)
@@ -564,15 +562,17 @@
 
     with jax.named_scope("frames"):
         for which in range(ITERS):
-            side_groups(which, 0, 1 + which)
-            side_groups(which, groups - which, groups + 1)
+            if which < ITERS - 1:
+                side_groups(which, 0, 1 + which)
+                side_groups(which, groups - which, groups + 1)
+            else:
+                side_groups(which, 0, groups + 1)
             for start, off in ends:
                 save(which, main, start, jnp.where(
                     off[None], 0.0, stage(which, main, start, beside_ring)))
 
     with jax.named_scope("moments"):
-        sums = side_sums(0, ITERS, [part[i] for i in range(2 * ITERS)])
-        sums = side_sums(groups - ITERS, groups, sums)
+        sums = side_sums(0, groups, [part[i] for i in range(2 * ITERS)])
         for (start, _), on in zip(ends, (line_t >= HALO, line_t < HALO)):
             new = products(main, start, right_ring, lambda p: jnp.where(on[None], keep_main(p), 0.0))
             sums = [s + fold(p) for s, p in zip(sums, new)]

time: 15.7 us -> 15.6 us (level)
  no operation moved by 1% of the time
where the time goes in v8:
time: 15.6 us; the launch traced here: 15.4 us
  Pallas kernels  14.8 us (95%)
  between operations  0.64 us (4%)
    pallas_call x1, Pallas kernels, per_device(): pl.pallas_call(functools.partial(gather_kernel, n_row, n_col, rows, cols,...  13.7 us
    pallas_call x1, Pallas kernels, per_device(): pl.pallas_call(functools.partial(finish_kernel, rows, cols), out_shape=(j...  1.02 us

profile of v8, /device:TPU:0, one launch (start us, length us, event | category | flops | bytes accessed | tf_op | source)
XLA Modules:
  0.0 15.4 jit_solution(138883732176982209)
XLA Ops:
  0.6 13.7 %shard_map.57 = (f32[3,9,144,128]{3,2,1,0:T(8,128)S(1)}, f32[3,4,64,128]{3,2,1,0:T(8,128)S(1)}, f32[3,2,256,128]{3,2,1,0:T(8,128)S(1)}, f32[3,8,128]{2,1,0:T(8,128)S(1)}) custom-call(f32[3,128,1024]{2,1,0:T(8,128)} %src_hbm.1, s32[128,1024]{1,0:T(8,128)} %lab_hbm.1), custom_call_target="tpu_custom_call" | custom-call | tf_op jit(solution)/shard_map/pallas_call | solution.py:776
  14.4 1.0 %shard_map.58 = (f32[128,1024]{1,0:T(8,128)}, f32[64,512]{1,0:T(8,128)}, f32[256,256]{1,0:T(8,128)}, f32[128,128]{1,0:T(8,128)}) custom-call(f32[3,9,144,128]{3,2,1,0:T(8,128)S(1)} %get-tuple-element.8.vec, f32[3,4,64,128]{3,2,1,0:T(8,128)S(1)} %get-tuple-element.9.fines, f32[3,2,256,128]{3,2,1,0:T(8,128)S(1)} %get-tuple-element.10.mids, ...), custom_call_target="tpu_custom_call" | custom-call | tf_op jit(solution)/shard_map/pallas_call | solution.py:820
